TPU v7x, 128 devices: a whole 4x4x4 slice. The times are simulated.
128 devices in a mesh: gx: 8 (over z, core), gy: 16 (over y, x).
Axes of the slice: x: 4, y: 4, z: 4, core: 2. Of those that a mesh axis runs over, the one named last changes fastest.
Arguments:
- gradient: float32 [64, 4096], P('gx', 'gy'), may hold values from -6 to 6
- warm_start: float32 [64, 4096], P('gx', 'gy'), may hold values from -3 to 3
- viscosity: float32 [32, 64, 4096], P(None, 'gx', 'gy'), may hold values from 1 to 10
- friction_coef: float32 [64, 4096], P('gx', 'gy'), may hold values from 0.5 to 5
- slide_dir: float32 [2, 64, 4096], P(None, 'gx', 'gy'), may hold values from -4 to 4
- obs_weight: float32 [64, 4096], P('gx', 'gy'), may hold values from 0.5 to 2
- ice_mask: int32 [64, 4096], P('gx', 'gy'), may hold values 0 or 1
- grounded: int32 [64, 4096], P('gx', 'gy'), may hold values 0 or 1
Outputs:
- solution: float32 [64, 4096], P('gx', 'gy')
- residual: float32 [64, 4096], P('gx', 'gy')
All inputs are finite; a program needn't handle non-finite values. No bound on the sum of `ice_mask` or of `grounded` on one device may be relied on, other than what follows from the above.
Results may differ from a plain program's by a relative error of at most 0.00075.
Values sent between devices are 32-bit elements; how exact they have to be, the bound alone decides.
A program may use at most 128 MiB of HBM per device.

v0:
```python
import jax
import jax.numpy as jnp
from jax import lax
from jax.sharding import Mesh
from jax.sharding import PartitionSpec as P

ITERS = 2
GX_GY = ("gx_0", "gx_1", "gy_0", "gy_1")
GX = ("gx_0", "gx_1")
GY = ("gy_0", "gy_1")


vert_coupling = 128.0
sink_rate = 0.0625
bed_drag = 0.5
offset_weight = 0.0019
cross_share = 0.5
reg_gamma = 0.02
reg_smooth = 1.0
diag_scale = 0.003
neighbour_offsets = [
    (step_z, step_x, step_y)
    for step_z in (-1, 0, 1)
    for step_x in (-1, 0, 1)
    for step_y in (-1, 0, 1)
    if step_x != 0 or step_y != 0
]


def by_axis(value, axes):
    for axis in axes:
        value = lax.psum(value, axis)
    return value


def extended(block, sides, width):
    for axis, dim in sides:
        count = lax.axis_size(axis)
        forward = [(i, i + 1) for i in range(count - 1)]
        backward = [(target, source) for source, target in forward]
        low = lax.ppermute(
            lax.slice_in_dim(block, block.shape[dim] - width, None, axis=dim), axis, forward
        )
        high = lax.ppermute(lax.slice_in_dim(block, 0, width, axis=dim), axis, backward)
        block = jnp.concatenate([low, block, high], axis=dim)
    return block


def couple(field_ext, eta_ext):
    levels = eta_ext.shape[0]
    span_x = eta_ext.shape[1] - 2
    span_y = eta_ext.shape[2] - 2
    padded_field = jnp.pad(field_ext, ((0, 0), (1, 1), (0, 0), (0, 0)))
    padded_eta = jnp.pad(eta_ext, ((1, 1), (0, 0), (0, 0)))
    center = eta_ext[:, 1 : 1 + span_x, 1 : 1 + span_y]
    along_one = jnp.zeros((levels, span_x, span_y), jnp.float32)
    along_two = jnp.zeros((levels, span_x, span_y), jnp.float32)
    for step_z, step_x, step_y in neighbour_offsets:
        near_eta = padded_eta[
            1 + step_z : 1 + step_z + levels,
            1 + step_x : 1 + step_x + span_x,
            1 + step_y : 1 + step_y + span_y,
        ]
        weight = (
            offset_weight / (abs(step_x) + abs(step_y) + abs(step_z)) * 0.5 * (center + near_eta)
        )
        near_field = padded_field[
            :,
            1 + step_z : 1 + step_z + levels,
            1 + step_x : 1 + step_x + span_x,
            1 + step_y : 1 + step_y + span_y,
        ]
        along_one = along_one + weight * near_field[0]
        along_two = along_two + weight * near_field[1]
        if step_x != 0 and step_y != 0:
            twist_weight = cross_share * step_x * step_y * weight
            along_one = along_one + twist_weight * near_field[1]
            along_two = along_two + twist_weight * near_field[0]
    return jnp.stack([along_one, along_two])


def tridiagonal(link_weights, diagonal, rhs_cols):
    levels = diagonal.shape[0]
    pivot_value = diagonal[0]
    ratios = [-link_weights[0] / pivot_value]
    partial_value = [rhs_cols[:, 0] / pivot_value]
    for layer_index in range(1, levels):
        pivot_value = diagonal[layer_index] + link_weights[layer_index - 1] * ratios[-1]
        partial_value.append(
            (rhs_cols[:, layer_index] + link_weights[layer_index - 1] * partial_value[-1])
            / pivot_value
        )
        if layer_index < levels - 1:
            ratios.append(-link_weights[layer_index] / pivot_value)
    result = [partial_value[-1]]
    for layer_index in range(levels - 2, -1, -1):
        result.insert(0, partial_value[layer_index] - ratios[layer_index] * result[0])
    return jnp.stack(result, axis=1)


def responses(viscosity, friction):
    levels = viscosity.shape[0]
    link_weights = vert_coupling * 0.5 * (viscosity[:-1] + viscosity[1:])
    zero_layer = jnp.zeros_like(viscosity[:1])
    diagonal = (
        jnp.concatenate([zero_layer, link_weights])
        + jnp.concatenate([link_weights, zero_layer])
        + sink_rate * viscosity
    )
    diagonal = diagonal.at[0].add(bed_drag * friction)
    unit_rhs = jnp.zeros((2,) + viscosity.shape, jnp.float32)
    unit_rhs = unit_rhs.at[0, 0].set(1.0).at[1, levels - 1].set(1.0)
    solved = tridiagonal(link_weights, diagonal, unit_rhs)
    return (solved[0], solved[1])


def regularize(centre_ext):
    middle = centre_ext[1:-1, 1:-1]
    beside_all = (
        centre_ext[2:, 1:-1] + centre_ext[:-2, 1:-1] + centre_ext[1:-1, 2:] + centre_ext[1:-1, :-2]
    )
    return reg_gamma * (middle + reg_smooth * (4.0 * middle - beside_all))


def paired_dots(residual, precond, image_vec):
    return (
        by_axis(jnp.sum(residual * precond), GX_GY),
        by_axis(jnp.sum(precond * image_vec), GX_GY),
    )


def on_device(
    gradient, warm_start, viscosity, friction_coef, slide_dir, obs_weight, ice_mask, grounded
):
    ice_float = ice_mask.astype(jnp.float32)
    ground_float = grounded.astype(jnp.float32)
    friction = ground_float * friction_coef
    source = (ice_float * ground_float * friction_coef)[None] * slide_dir
    obs = ice_float * obs_weight
    inverse_diag = 1.0 / (
        reg_gamma * (1.0 + 4.0 * reg_smooth)
        + diag_scale * ice_float * ground_float * friction_coef * friction_coef
    )
    viscosity_wide = extended(viscosity, ((GX, 1), (GY, 2)), 2)
    columns = jnp.concatenate([source, obs[None], friction[None]], axis=0)
    column_wide = extended(columns, ((GX, 1), (GY, 2)), 2)
    safe_eta = jnp.where(viscosity_wide > 0.0, viscosity_wide, 1.0)
    bottom_wide, top_wide = responses(safe_eta, column_wide[3])
    bottom_inner = bottom_wide[:, 1:-1, 1:-1]
    top_inner = top_wide[:, 1:-1, 1:-1]
    bottom_own = bottom_wide[:, 2:-2, 2:-2]
    top_own = top_wide[:, 2:-2, 2:-2]

    def hessian(direction):
        wide_dir = extended(direction, ((GX, 0), (GY, 1)), 2)
        spread = column_wide[:2] * wide_dir[None]
        first_state = bottom_wide[None] * spread[:, None]
        coupled = couple(first_state, viscosity_wide)
        surface = spread[:, 1:-1, 1:-1] * bottom_inner[-1][None] + jnp.sum(
            top_inner[None] * coupled, axis=1
        )
        traction = column_wide[2, 1:-1, 1:-1][None] * surface
        second_state = top_inner[None] * traction[:, None]
        coupled_back = couple(second_state, viscosity_wide[:, 1:-1, 1:-1])
        basal_part = traction[:, 1:-1, 1:-1] * top_own[0][None] + jnp.sum(
            bottom_own[None] * coupled_back, axis=1
        )
        return jnp.sum(source * basal_part, axis=0) + regularize(wide_dir[1:-1, 1:-1])

    solution = warm_start
    residual = gradient - hessian(warm_start)
    precond = inverse_diag * residual
    image_vec = hessian(precond)
    norm_now, product = paired_dots(residual, precond, image_vec)
    step_size = norm_now / product
    direction = precond
    along_dir = image_vec
    for iteration in range(ITERS):
        solution = solution + step_size * direction
        residual = residual - step_size * along_dir
        if iteration + 1 < ITERS:
            precond = inverse_diag * residual
            image_vec = hessian(precond)
            norm_next, product = paired_dots(residual, precond, image_vec)
            ratio_cg = norm_next / norm_now
            step_size = norm_next / (product - ratio_cg * norm_next / step_size)
            direction = precond + ratio_cg * direction
            along_dir = image_vec + ratio_cg * along_dir
            norm_now = norm_next
    return (solution, residual)


def solution(mesh):
    finer = Mesh(mesh.devices.reshape(4, 2, 4, 4), ("gx_0", "gx_1", "gy_0", "gy_1"))
    return jax.shard_map(
        on_device,
        mesh=finer,
        in_specs=(
            P(GX, GY),
            P(GX, GY),
            P(None, GX, GY),
            P(GX, GY),
            P(None, GX, GY),
            P(GX, GY),
            P(GX, GY),
            P(GX, GY),
        ),
        out_specs=(P(GX, GY), P(GX, GY)),
        check_vma=False,
    )
```

profile of v0, /device:TPU:1, one launch (start us, length us, event | category | flops | bytes accessed | tf_op | source)
XLA Modules:
  0.0 276.2 jit_solution(12042140770638936635)
XLA Ops:
  1.4 4.9 %collective-permute-start.4 = (f32[2,256]{1,0:T(2,128)S(1)}, f32[2,256]{1,0:T(2,128)S(1)}, u32[]{:S(2)}, u32[]{:S(2)}) collective-permute-start(f32[2,256]{1,0:T(2,128)S(1)} %get-tuple-element.261), channel_id=1, source_target_pairs={{0,16},{16,32},{32,48},{48,64},{64,80},{80,96},{96,112},{1,17},{17... | collective-permute-start | bytes 6152 | tf_op jit(solution)/shard_map/ppermute | solution.py:41
  6.3 1.9 collective-permute-start.5
  9.8 3.8 %collective-permute-start = (f32[4,2,256]{2,1,0:T(2,128)S(1)}, f32[4,2,256]{2,1,0:T(2,128)S(1)}, u32[]{:S(2)}, u32[]{:S(2)}) collective-permute-start(f32[4,2,256]{2,1,0:T(2,128)S(1)} %get-tuple-element.246), channel_id=1, source_target_pairs={{0,16},{16,32},{32,48},{48,64},{64,80},{80,96},{96,112},{1,17},{17... | collective-permute-start | bytes 24584 | tf_op jit(solution)/shard_map/ppermute | solution.py:41
  13.5 1.9 collective-permute-start.1
  15.5 1.1 fusion.622
  16.5 3.6 %collective-permute-start.8 = (f32[32,2,256]{2,1,0:T(2,128)S(1)}, f32[32,2,256]{2,1,0:T(2,128)S(1)}, u32[]{:S(2)}, u32[]{:S(2)}) collective-permute-start(f32[32,2,256]{2,1,0:T(2,128)S(1)} %get-tuple-element.242), channel_id=1, source_target_pairs={{0,16},{16,32},{32,48},{48,64},{64,80},{80,96},{96,112},{1,17},{17... | collective-permute-start | bytes 196616 | tf_op jit(solution)/shard_map/ppermute | solution.py:41
  20.2 1.9 collective-permute-start.9
  22.9 3.1 %collective-permute-start.6 = (f32[12,2]{1,0:T(8,128)S(1)}, f32[12,2]{1,0:T(8,128)S(1)}, u32[]{:S(2)}, u32[]{:S(2)}) collective-permute-start(f32[12,2]{1,0:T(8,128)S(1)} %get-tuple-element.252), channel_id=1, source_target_pairs={{0,1},{1,2},{2,3},{3,4},{4,5},{5,6},{6,7},{7,8},{8,9},{9,10},{10,1... | collective-permute-start | bytes 296 | tf_op jit(solution)/shard_map/ppermute | solution.py:41
  26.1 1.3 collective-permute-start.7
  27.5 4.0 %collective-permute-start.2 = (f32[4,12,2]{2,1,0:T(8,128)S(1)}, f32[4,12,2]{2,1,0:T(8,128)S(1)}, u32[]{:S(2)}, u32[]{:S(2)}) collective-permute-start(f32[4,12,2]{2,1,0:T(8,128)S(1)} %get-tuple-element.244), channel_id=1, source_target_pairs={{0,1},{1,2},{2,3},{3,4},{4,5},{5,6},{6,7},{7,8},{8,9},{9,10},{10,1... | collective-permute-start | bytes 1160 | tf_op jit(solution)/shard_map/ppermute | solution.py:41
  31.5 1.3 collective-permute-start.3
  33.6 2.5 collective-permute-done.3
  36.9 1.0 pad_maximum_fusion.2
  38.1 3.1 %collective-permute-start.10 = (f32[32,12,2]{2,1,0:T(8,128)S(1)}, f32[32,12,2]{2,1,0:T(8,128)S(1)}, u32[]{:S(2)}, u32[]{:S(2)}) collective-permute-start(f32[32,12,2]{2,1,0:T(8,128)S(1)} %get-tuple-element.238), channel_id=1, source_target_pairs={{0,1},{1,2},{2,3},{3,4},{4,5},{5,6},{6,7},{7,8},{8,9},{9,10},{10,1... | collective-permute-start | bytes 9224 | tf_op jit(solution)/shard_map/ppermute | solution.py:41
  41.3 1.3 collective-permute-start.11
  43.2 3.5 %collective-permute-done.10 = f32[32,12,2]{2,1,0:T(8,128)S(1)} collective-permute-done((f32[32,12,2]{2,1,0:T(8,128)S(1)}, f32[32,12,2]{2,1,0:T(8,128)S(1)}, u32[]{:S(2)}, u32[]{:S(2)}) %collective-permute-start.10) | collective-permute-done | bytes 3104 | tf_op jit(solution)/shard_map/ppermute | solution.py:41
  46.7 5.7 %collective-permute-done.11 = f32[32,12,2]{2,1,0:T(8,128)S(1)} collective-permute-done((f32[32,12,2]{2,1,0:T(8,128)S(1)}, f32[32,12,2]{2,1,0:T(8,128)S(1)}, u32[]{:S(2)}, u32[]{:S(2)}) %collective-permute-start.11) | collective-permute-done | bytes 3104 | tf_op jit(solution)/shard_map/ppermute | solution.py:44
  53.4 1.2 slice.2865
  59.5 9.6 %fusion.241 = (f32[1,32,10,258]{3,2,1,0:T(8,128)}, f32[32,10,258]{2,1,0:T(8,128)S(1)}, f32[32,10,258]{2,1,0:T(8,128)S(1)}, f32[32,10,258]{2,1,0:T(8,128)S(1)}, f...) fusion(f32[2,32,12,260]{3,2,1,0:T(8,128)S(1)} %broadcast_multip, ...), kind=kLoop, calls=%fused_computation.521 | loop fusion | flops 10815360 | bytes 27130368 | tf_op jit(solution)/shard_map/stack | solution.py:79
  69.2 9.7 %fusion.242 = f32[1,32,10,258]{3,2,1,0:T(8,128)} fusion(f32[32,10,258]{2,1,0:T(8,128)} %get-tuple-element.109, f32[32,10,258]{2,1,0:T(8,128)} %get-tuple-element.108, f32[32,10,258]{2,1,0:T(8,128)} %get-tuple-element.107, f32[32,10,258]{2,1,0:T(8,128)} %get-tuple-element.106, f32[32,10,258]{2,1,0:T(8,128)} %get-tuple-element.105, ...), kind=kLoop, calls=%fused_computation.522 | loop fusion | flops 7843200 | bytes 22459392 | tf_op jit(solution)/shard_map/stack | solution.py:79
  78.9 1.6 fusion
  82.2 4.4 %fusion.518 = (f32[1,32,8,256]{3,2,1,0:T(8,128)}, f32[32,8,256]{2,1,0:T(8,128)}, f32[32,8,256]{2,1,0:T(8,128)}, f32[32,8,256]{2,1,0:T(8,128)}, f32[32,8,256]{2,1...) fusion(f32[2,32,10,258]{3,2,1,0:T(8,128)S(1)} %broadcast_multip, ...), kind=kLoop, calls=%fused_computation.1103 | loop fusion | flops 8716288 | bytes 13500416 | tf_op jit(solution)/shard_map/stack | solution.py:79
  86.6 4.5 %fusion.515 = f32[1,32,8,256]{3,2,1,0:T(8,128)} fusion(f32[32,8,256]{2,1,0:T(8,128)} %get-tuple-element.84, f32[32,8,256]{2,1,0:T(8,128)} %get-tuple-element.83, f32[32,8,256]{2,1,0:T(8,128)} %get-tuple-element.82, f32[32,8,256]{2,1,0:T(8,128)} %get-tuple-element.81, f32[2,32,10,258]{3,2,1,0:T(8,128)S(1)} %broadcast_multiply_fusion.4, ...), kind=kLoop, calls=%fused_computation.1100 | loop fusion | flops 6619136 | bytes 11141120 | tf_op jit(solution)/shard_map/stack | solution.py:79
  91.2 1.2 fusion.248
  92.4 1.0 fusion.537
  93.5 1.6 fusion.594
  95.1 4.1 %collective-permute-start.12 = (f32[2,256]{1,0:T(2,128)S(1)}, f32[2,256]{1,0:T(2,128)S(1)}, u32[]{:S(2)}, u32[]{:S(2)}) collective-permute-start(f32[2,256]{1,0:T(2,128)S(1)} %get-tuple-element.259), channel_id=1, source_target_pairs={{0,16},{16,32},{32,48},{48,64},{64,80},{80,96},{96,112},{1,17},{17... | collective-permute-start | bytes 6152 | tf_op jit(solution)/shard_map/ppermute | solution.py:41
  99.2 1.9 collective-permute-start.13
  101.2 3.0 %collective-permute-done.13 = f32[2,256]{1,0:T(2,128)S(1)} collective-permute-done((f32[2,256]{1,0:T(2,128)S(1)}, f32[2,256]{1,0:T(2,128)S(1)}, u32[]{:S(2)}, u32[]{:S(2)}) %collective-permute-start.13) | collective-permute-done | bytes 2080 | tf_op jit(solution)/shard_map/ppermute | solution.py:44
  104.2 5.5 %collective-permute-start.14 = (f32[12,2]{1,0:T(8,128)S(1)}, f32[12,2]{1,0:T(8,128)S(1)}, u32[]{:S(2)}, u32[]{:S(2)}) collective-permute-start(f32[12,2]{1,0:T(8,128)S(1)} %get-tuple-element.250), channel_id=1, source_target_pairs={{0,1},{1,2},{2,3},{3,4},{4,5},{5,6},{6,7},{7,8},{8,9},{9,10},{10,1... | collective-permute-start | bytes 296 | tf_op jit(solution)/shard_map/ppermute | solution.py:41
  109.7 1.5 collective-permute-start.15
  111.2 3.2 %collective-permute-done.15 = f32[12,2]{1,0:T(8,128)S(1)} collective-permute-done((f32[12,2]{1,0:T(8,128)S(1)}, f32[12,2]{1,0:T(8,128)S(1)}, u32[]{:S(2)}, u32[]{:S(2)}) %collective-permute-start.15) | collective-permute-done | bytes 128 | tf_op jit(solution)/shard_map/ppermute | solution.py:44
  116.4 1.2 broadcast_multiply_fusion.3
  117.7 8.7 %fusion.244 = f32[1,32,10,258]{3,2,1,0:T(8,128)} fusion(f32[32,10,258]{2,1,0:T(8,128)} %get-tuple-element.109, f32[32,10,258]{2,1,0:T(8,128)} %get-tuple-element.108, f32[32,10,258]{2,1,0:T(8,128)} %get-tuple-element.107, f32[32,10,258]{2,1,0:T(8,128)} %get-tuple-element.106, f32[32,10,258]{2,1,0:T(8,128)} %get-tuple-element.105, ...), kind=kLoop, calls=%fused_computation.524 | loop fusion | flops 7843200 | bytes 22459392 | tf_op jit(solution)/shard_map/stack | solution.py:79
  126.4 8.6 %fusion.243 = f32[1,32,10,258]{3,2,1,0:T(8,128)} fusion(f32[32,10,258]{2,1,0:T(8,128)} %get-tuple-element.109, f32[32,10,258]{2,1,0:T(8,128)} %get-tuple-element.108, f32[32,10,258]{2,1,0:T(8,128)} %get-tuple-element.107, f32[32,10,258]{2,1,0:T(8,128)} %get-tuple-element.106, f32[32,10,258]{2,1,0:T(8,128)} %get-tuple-element.105, ...), kind=kLoop, calls=%fused_computation.523 | loop fusion | flops 7843200 | bytes 22459392 | tf_op jit(solution)/shard_map/stack | solution.py:79
  135.0 1.6 fusion.1
  137.5 4.5 %fusion.516 = f32[1,32,8,256]{3,2,1,0:T(8,128)} fusion(f32[32,8,256]{2,1,0:T(8,128)} %get-tuple-element.84, f32[32,8,256]{2,1,0:T(8,128)} %get-tuple-element.83, f32[32,8,256]{2,1,0:T(8,128)} %get-tuple-element.82, f32[32,8,256]{2,1,0:T(8,128)} %get-tuple-element.81, f32[2,32,10,258]{3,2,1,0:T(8,128)S(1)} %broadcast_multiply_fusion.2, ...), kind=kLoop, calls=%fused_computation.1101 | loop fusion | flops 6619136 | bytes 11141120 | tf_op jit(solution)/shard_map/stack | solution.py:79
  142.0 4.5 %fusion.519 = f32[1,32,8,256]{3,2,1,0:T(8,128)} fusion(f32[32,8,256]{2,1,0:T(8,128)} %get-tuple-element.84, f32[2,32,10,258]{3,2,1,0:T(8,128)S(1)} %broadcast_multiply_fusion.2, f32[32,8,256]{2,1,0:T(8,128)} %get-tuple-element.83, f32[32,8,256]{2,1,0:T(8,128)} %get-tuple-element.82, f32[32,8,256]{2,1,0:T(8,128)} %get-tuple-element.81, ...), kind=kLoop, calls=%fused_computation.1104 | loop fusion | flops 6619136 | bytes 11141120 | tf_op jit(solution)/shard_map/stack | solution.py:79
  146.5 1.2 fusion.249
  148.6 2.1 multiply_reduce_fusion.2
  150.7 8.3 %all-reduce.15 = (f32[]{:T(128)}, f32[]{:T(128)}) all-reduce(f32[]{:T(128)} %get-tuple-element.41, f32[]{:T(128)} %get-tuple-element.40), channel_id=1, replica_groups=mesh['gx_0'=4,'gx_1'=2,'gy_0'=4,'gy_1'=4] {'gx_0'}, use_global_device_ids=true, to_apply=%region_4.5 | all-reduce | flops 2 | bytes 16 | tf_op jit(solution)/shard_map/psum | solution.py:32
  158.9 6.6 %all-reduce.17 = (f32[]{:T(128)}, f32[]{:T(128)}) all-reduce(f32[]{:T(128)} %get-tuple-element.52, f32[]{:T(128)} %get-tuple-element.53), channel_id=1, replica_groups=mesh['gx_0'=4,'gx_1'=2,'gy_0'=4,'gy_1'=4] {'gx_1'}, use_global_device_ids=true, to_apply=%region_5.6 | all-reduce | flops 2 | bytes 16 | tf_op jit(solution)/shard_map/psum | solution.py:32
  165.5 9.7 %all-reduce.13 = (f32[]{:T(128)}, f32[]{:T(128)}) all-reduce(f32[]{:T(128)} %get-tuple-element.56, f32[]{:T(128)} %get-tuple-element.57), channel_id=1, replica_groups=mesh['gx_0'=4,'gx_1'=2,'gy_0'=4,'gy_1'=4] {'gy_0'}, use_global_device_ids=true, to_apply=%region_6.7 | all-reduce | flops 2 | bytes 16 | tf_op jit(solution)/shard_map/psum | solution.py:32
  175.3 9.4 %all-reduce.11 = (f32[]{:T(128)}, f32[]{:T(128)}) all-reduce(f32[]{:T(128)} %get-tuple-element.48, f32[]{:T(128)} %get-tuple-element.49), channel_id=1, replica_groups=mesh['gx_0'=4,'gx_1'=2,'gy_0'=4,'gy_1'=4] {'gy_1'}, use_global_device_ids=true, to_apply=%region_7.8 | all-reduce | flops 2 | bytes 16 | tf_op jit(solution)/shard_map/psum | solution.py:32
  186.0 0.9 fusion.562
  186.9 5.1 %collective-permute-start.16 = (f32[2,256]{1,0:T(2,128)S(1)}, f32[2,256]{1,0:T(2,128)S(1)}, u32[]{:S(2)}, u32[]{:S(2)}) collective-permute-start(f32[2,256]{1,0:T(2,128)S(1)} %get-tuple-element.257), channel_id=1, source_target_pairs={{0,16},{16,32},{32,48},{48,64},{64,80},{80,96},{96,112},{1,17},{17... | collective-permute-start | bytes 6152 | tf_op jit(solution)/shard_map/ppermute | solution.py:41
  192.0 2.5 collective-permute-start.17
  194.5 2.4 collective-permute-done.17
  197.0 1.3 collective-permute-start.18
  198.3 1.5 collective-permute-start.19
  199.8 2.9 %collective-permute-done.19 = f32[12,2]{1,0:T(8,128)S(1)} collective-permute-done((f32[12,2]{1,0:T(8,128)S(1)}, f32[12,2]{1,0:T(8,128)S(1)}, u32[]{:S(2)}, u32[]{:S(2)}) %collective-permute-start.19) | collective-permute-done | bytes 128 | tf_op jit(solution)/shard_map/ppermute | solution.py:44
  204.2 1.2 broadcast_multiply_fusion.1
  205.5 8.8 %fusion.246 = f32[1,32,10,258]{3,2,1,0:T(8,128)} fusion(f32[32,10,258]{2,1,0:T(8,128)} %get-tuple-element.109, f32[32,10,258]{2,1,0:T(8,128)} %get-tuple-element.108, f32[32,10,258]{2,1,0:T(8,128)} %get-tuple-element.107, f32[32,10,258]{2,1,0:T(8,128)} %get-tuple-element.106, f32[32,10,258]{2,1,0:T(8,128)} %get-tuple-element.105, ...), kind=kLoop, calls=%fused_computation.526 | loop fusion | flops 7843200 | bytes 22003200 | tf_op jit(solution)/shard_map/stack | solution.py:79
  214.3 8.6 %fusion.245 = f32[1,32,10,258]{3,2,1,0:T(8,128)} fusion(f32[32,10,258]{2,1,0:T(8,128)} %get-tuple-element.109, f32[32,10,258]{2,1,0:T(8,128)} %get-tuple-element.108, f32[32,10,258]{2,1,0:T(8,128)} %get-tuple-element.107, f32[32,10,258]{2,1,0:T(8,128)} %get-tuple-element.106, f32[32,10,258]{2,1,0:T(8,128)} %get-tuple-element.105, ...), kind=kLoop, calls=%fused_computation.525 | loop fusion | flops 7843200 | bytes 22459392 | tf_op jit(solution)/shard_map/stack | solution.py:79
  223.0 1.6 fusion.2
  226.3 4.1 %fusion.517 = f32[1,32,8,256]{3,2,1,0:T(8,128)} fusion(f32[32,8,256]{2,1,0:T(8,128)} %get-tuple-element.84, f32[32,8,256]{2,1,0:T(8,128)} %get-tuple-element.83, f32[32,8,256]{2,1,0:T(8,128)} %get-tuple-element.82, f32[32,8,256]{2,1,0:T(8,128)} %get-tuple-element.81, f32[2,32,10,258]{3,2,1,0:T(8,128)S(1)} %broadcast_multiply_fusion, ...), kind=kLoop, calls=%fused_computation.1102 | loop fusion | flops 6619136 | bytes 11141120 | tf_op jit(solution)/shard_map/stack | solution.py:79
  230.4 4.0 %fusion.520 = f32[1,32,8,256]{3,2,1,0:T(8,128)} fusion(f32[32,8,256]{2,1,0:T(8,128)} %get-tuple-element.84, f32[2,32,10,258]{3,2,1,0:T(8,128)S(1)} %broadcast_multiply_fusion, f32[32,8,256]{2,1,0:T(8,128)} %get-tuple-element.83, f32[32,8,256]{2,1,0:T(8,128)} %get-tuple-element.82, f32[32,8,256]{2,1,0:T(8,128)} %get-tuple-element.81, ...), kind=kLoop, calls=%fused_computation.1105 | loop fusion | flops 6619136 | bytes 11141120 | tf_op jit(solution)/shard_map/stack | solution.py:79
  234.5 1.2 fusion.250
  236.5 1.5 multiply_reduce_fusion
  238.0 7.9 %all-reduce.14 = (f32[]{:T(128)}, f32[]{:T(128)}) all-reduce(f32[]{:T(128)} %get-tuple-element.39, f32[]{:T(128)} %get-tuple-element.38), channel_id=1, replica_groups=mesh['gx_0'=4,'gx_1'=2,'gy_0'=4,'gy_1'=4] {'gx_0'}, use_global_device_ids=true, to_apply=%region_17.18 | all-reduce | flops 2 | bytes 16 | tf_op jit(solution)/shard_map/psum | solution.py:32
  246.0 5.3 %all-reduce.16 = (f32[]{:T(128)}, f32[]{:T(128)}) all-reduce(f32[]{:T(128)} %get-tuple-element.50, f32[]{:T(128)} %get-tuple-element.51), channel_id=1, replica_groups=mesh['gx_0'=4,'gx_1'=2,'gy_0'=4,'gy_1'=4] {'gx_1'}, use_global_device_ids=true, to_apply=%region_18.19 | all-reduce | flops 2 | bytes 16 | tf_op jit(solution)/shard_map/psum | solution.py:32
  251.2 9.5 %all-reduce.12 = (f32[]{:T(128)}, f32[]{:T(128)}) all-reduce(f32[]{:T(128)} %get-tuple-element.54, f32[]{:T(128)} %get-tuple-element.55), channel_id=1, replica_groups=mesh['gx_0'=4,'gx_1'=2,'gy_0'=4,'gy_1'=4] {'gy_0'}, use_global_device_ids=true, to_apply=%region_19.20 | all-reduce | flops 2 | bytes 16 | tf_op jit(solution)/shard_map/psum | solution.py:32
  260.7 9.6 %all-reduce.10 = (f32[]{:T(128)}, f32[]{:T(128)}) all-reduce(f32[]{:T(128)} %get-tuple-element.46, f32[]{:T(128)} %get-tuple-element.47), channel_id=1, replica_groups=mesh['gx_0'=4,'gx_1'=2,'gy_0'=4,'gy_1'=4] {'gy_1'}, use_global_device_ids=true, to_apply=%region_20.21 | all-reduce | flops 2 | bytes 16 | tf_op jit(solution)/shard_map/psum | solution.py:32
  274.8 1.4 multiply_subtract_fusion.30
  (236 shorter events, 20.4 us)
Async XLA Ops:
  1.4 18.8 %collective-permute-start.4 = (f32[2,256]{1,0:T(2,128)S(1)}, f32[2,256]{1,0:T(2,128)S(1)}, u32[]{:S(2)}, u32[]{:S(2)}) collective-permute-start(f32[2,256]{1,0:T(2,128)S(1)} %get-tuple-element.261), channel_id=1, source_target_pairs={{0,16},{16,32},{32,48},{48,64},{64,80},{80,96},{96,112},{1,17},{17... | collective-permute-start | bytes 6152 | tf_op jit(solution)/shard_map/ppermute | solution.py:41
  6.3 15.8 %collective-permute-start.5 = (f32[2,256]{1,0:T(2,128)S(1)}, f32[2,256]{1,0:T(2,128)S(1)}, u32[]{:S(2)}, u32[]{:S(2)}) collective-permute-start(f32[2,256]{1,0:T(2,128)S(1)} %get-tuple-element.262), channel_id=1, source_target_pairs={{16,0},{32,16},{48,32},{64,48},{80,64},{96,80},{112,96},{17,1},{33... | collective-permute-start | bytes 6152 | tf_op jit(solution)/shard_map/ppermute | solution.py:44
  9.0 83.4 %copy-start.51 = (f32[8,256]{1,0:T(8,128)}, f32[8,256]{1,0:T(8,128)S(1)}, u32[]{:S(2)}) copy-start(f32[8,256]{1,0:T(8,128)S(1)} %get-tuple-element.255) | copy-start | bytes 24580
  9.7 42.7 %copy-start.12 = (f32[32,8,256]{2,1,0:T(8,128)S(1)}, f32[32,8,256]{2,1,0:T(8,128)}, u32[]{:S(2)}) copy-start(f32[32,8,256]{2,1,0:T(8,128)} %param.16) | copy-start | bytes 786436
  9.8 16.3 %collective-permute-start = (f32[4,2,256]{2,1,0:T(2,128)S(1)}, f32[4,2,256]{2,1,0:T(2,128)S(1)}, u32[]{:S(2)}, u32[]{:S(2)}) collective-permute-start(f32[4,2,256]{2,1,0:T(2,128)S(1)} %get-tuple-element.246), channel_id=1, source_target_pairs={{0,16},{16,32},{32,48},{48,64},{64,80},{80,96},{96,112},{1,17},{17... | collective-permute-start | bytes 24584 | tf_op jit(solution)/shard_map/ppermute | solution.py:41
  13.5 13.8 %collective-permute-start.1 = (f32[4,2,256]{2,1,0:T(2,128)S(1)}, f32[4,2,256]{2,1,0:T(2,128)S(1)}, u32[]{:S(2)}, u32[]{:S(2)}) collective-permute-start(f32[4,2,256]{2,1,0:T(2,128)S(1)} %get-tuple-element.247), channel_id=1, source_target_pairs={{16,0},{32,16},{48,32},{64,48},{80,64},{96,80},{112,96},{17,1},{33... | collective-permute-start | bytes 24584 | tf_op jit(solution)/shard_map/ppermute | solution.py:44
  16.5 19.8 %collective-permute-start.8 = (f32[32,2,256]{2,1,0:T(2,128)S(1)}, f32[32,2,256]{2,1,0:T(2,128)S(1)}, u32[]{:S(2)}, u32[]{:S(2)}) collective-permute-start(f32[32,2,256]{2,1,0:T(2,128)S(1)} %get-tuple-element.242), channel_id=1, source_target_pairs={{0,16},{16,32},{32,48},{48,64},{64,80},{80,96},{96,112},{1,17},{17... | collective-permute-start | bytes 196616 | tf_op jit(solution)/shard_map/ppermute | solution.py:41
  20.2 32.8 %copy-start.60 = (f32[2,256]{1,0:T(2,128)}, f32[2,256]{1,0:T(2,128)S(1)}, u32[]{:S(2)}) copy-start(f32[2,256]{1,0:T(2,128)S(1)} %collective-permute-done.4) | copy-start | bytes 6148
  20.2 16.7 %collective-permute-start.9 = (f32[32,2,256]{2,1,0:T(2,128)S(1)}, f32[32,2,256]{2,1,0:T(2,128)S(1)}, u32[]{:S(2)}, u32[]{:S(2)}) collective-permute-start(f32[32,2,256]{2,1,0:T(2,128)S(1)} %get-tuple-element.243), channel_id=1, source_target_pairs={{16,0},{32,16},{48,32},{64,48},{80,64},{96,80},{112,96},{17,1},{33... | collective-permute-start | bytes 196616 | tf_op jit(solution)/shard_map/ppermute | solution.py:44
  22.2 30.9 %copy-start.62 = (f32[2,256]{1,0:T(2,128)}, f32[2,256]{1,0:T(2,128)S(1)}, u32[]{:S(2)}) copy-start(f32[2,256]{1,0:T(2,128)S(1)} %collective-permute-done.5) | copy-start | bytes 6148
  22.9 8.5 %collective-permute-start.6 = (f32[12,2]{1,0:T(8,128)S(1)}, f32[12,2]{1,0:T(8,128)S(1)}, u32[]{:S(2)}, u32[]{:S(2)}) collective-permute-start(f32[12,2]{1,0:T(8,128)S(1)} %get-tuple-element.252), channel_id=1, source_target_pairs={{0,1},{1,2},{2,3},{3,4},{4,5},{5,6},{6,7},{7,8},{8,9},{9,10},{10,1... | collective-permute-start | bytes 296 | tf_op jit(solution)/shard_map/ppermute | solution.py:41
  26.1 6.7 %collective-permute-start.7 = (f32[12,2]{1,0:T(8,128)S(1)}, f32[12,2]{1,0:T(8,128)S(1)}, u32[]{:S(2)}, u32[]{:S(2)}) collective-permute-start(f32[12,2]{1,0:T(8,128)S(1)} %get-tuple-element.253), channel_id=1, source_target_pairs={{1,0},{2,1},{3,2},{4,3},{5,4},{6,5},{7,6},{8,7},{9,8},{10,9},{11,1... | collective-permute-start | bytes 296 | tf_op jit(solution)/shard_map/ppermute | solution.py:44
  27.5 6.1 %collective-permute-start.2 = (f32[4,12,2]{2,1,0:T(8,128)S(1)}, f32[4,12,2]{2,1,0:T(8,128)S(1)}, u32[]{:S(2)}, u32[]{:S(2)}) collective-permute-start(f32[4,12,2]{2,1,0:T(8,128)S(1)} %get-tuple-element.244), channel_id=1, source_target_pairs={{0,1},{1,2},{2,3},{3,4},{4,5},{5,6},{6,7},{7,8},{8,9},{9,10},{10,1... | collective-permute-start | bytes 1160 | tf_op jit(solution)/shard_map/ppermute | solution.py:41
  31.5 21.6 %copy-start.58 = (f32[12,2]{1,0:T(8,128)}, f32[12,2]{1,0:T(8,128)S(1)}, u32[]{:S(2)}) copy-start(f32[12,2]{1,0:T(8,128)S(1)} %collective-permute-done.6) | copy-start | bytes 292
  31.5 4.7 %collective-permute-start.3 = (f32[4,12,2]{2,1,0:T(8,128)S(1)}, f32[4,12,2]{2,1,0:T(8,128)S(1)}, u32[]{:S(2)}, u32[]{:S(2)}) collective-permute-start(f32[4,12,2]{2,1,0:T(8,128)S(1)} %get-tuple-element.245), channel_id=1, source_target_pairs={{1,0},{2,1},{3,2},{4,3},{5,4},{6,5},{7,6},{8,7},{9,8},{10,9},{11,1... | collective-permute-start | bytes 1160 | tf_op jit(solution)/shard_map/ppermute | solution.py:44
  32.8 20.3 %copy-start.59 = (f32[12,2]{1,0:T(8,128)}, f32[12,2]{1,0:T(8,128)S(1)}, u32[]{:S(2)}) copy-start(f32[12,2]{1,0:T(8,128)S(1)} %collective-permute-done.7) | copy-start | bytes 292
  36.3 22.5 %copy-start.32 = (f32[2,12,260]{2,1,0:T(8,128)}, f32[2,12,260]{2,1,0:T(8,128)S(1)}, u32[]{:S(2)}) copy-start(f32[2,12,260]{2,1,0:T(8,128)S(1)} %slice_multiply_fusion.5) | copy-start | bytes 74884
  38.1 8.6 %collective-permute-start.10 = (f32[32,12,2]{2,1,0:T(8,128)S(1)}, f32[32,12,2]{2,1,0:T(8,128)S(1)}, u32[]{:S(2)}, u32[]{:S(2)}) collective-permute-start(f32[32,12,2]{2,1,0:T(8,128)S(1)} %get-tuple-element.238), channel_id=1, source_target_pairs={{0,1},{1,2},{2,3},{3,4},{4,5},{5,6},{6,7},{7,8},{8,9},{9,10},{10,1... | collective-permute-start | bytes 9224 | tf_op jit(solution)/shard_map/ppermute | solution.py:41
  41.3 11.2 %collective-permute-start.11 = (f32[32,12,2]{2,1,0:T(8,128)S(1)}, f32[32,12,2]{2,1,0:T(8,128)S(1)}, u32[]{:S(2)}, u32[]{:S(2)}) collective-permute-start(f32[32,12,2]{2,1,0:T(8,128)S(1)} %get-tuple-element.239), channel_id=1, source_target_pairs={{1,0},{2,1},{3,2},{4,3},{5,4},{6,5},{7,6},{8,7},{9,8},{10,9},{11,1... | collective-permute-start | bytes 9224 | tf_op jit(solution)/shard_map/ppermute | solution.py:44
  56.8 2.1 copy-start.17
  58.0 22.5 %copy-start.38 = (f32[10,258]{1,0:T(8,128)}, f32[10,258]{1,0:T(8,128)S(1)}, u32[]{:S(2)}) copy-start(f32[10,258]{1,0:T(8,128)S(1)} %slice_bitcast_fusion.98) | copy-start | bytes 30964
  59.5 9.6 %copy-start.13 = (f32[32,12,258]{2,1,0:T(8,128)}, f32[32,12,258]{2,1,0:T(8,128)S(1)}, u32[]{:S(2)}) copy-start(f32[32,12,258]{2,1,0:T(8,128)S(1)} %get-tuple-element.240) | copy-start | bytes 1188868
  59.5 9.6 %copy-start.15 = (f32[32,12,258]{2,1,0:T(8,128)}, f32[32,12,258]{2,1,0:T(8,128)S(1)}, u32[]{:S(2)}) copy-start(f32[32,12,258]{2,1,0:T(8,128)S(1)} %get-tuple-element.241) | copy-start | bytes 1188868
  69.1 9.8 %copy-start = (f32[32,10,258]{2,1,0:T(8,128)}, f32[32,10,258]{2,1,0:T(8,128)S(1)}, u32[]{:S(2)}) copy-start(f32[32,10,258]{2,1,0:T(8,128)S(1)} %get-tuple-element.89) | copy-start | bytes 990724
  69.1 9.8 %copy-start.3 = (f32[32,10,258]{2,1,0:T(8,128)}, f32[32,10,258]{2,1,0:T(8,128)S(1)}, u32[]{:S(2)}) copy-start(f32[32,10,258]{2,1,0:T(8,128)S(1)} %get-tuple-element.90) | copy-start | bytes 990724
  69.1 9.8 %copy-start.6 = (f32[32,10,258]{2,1,0:T(8,128)}, f32[32,10,258]{2,1,0:T(8,128)S(1)}, u32[]{:S(2)}) copy-start(f32[32,10,258]{2,1,0:T(8,128)S(1)} %get-tuple-element.91) | copy-start | bytes 990724
  69.2 9.8 %copy-start.9 = (f32[32,10,258]{2,1,0:T(8,128)}, f32[32,10,258]{2,1,0:T(8,128)S(1)}, u32[]{:S(2)}) copy-start(f32[32,10,258]{2,1,0:T(8,128)S(1)} %get-tuple-element.92) | copy-start | bytes 990724
  78.9 1.6 copy-start.33
  80.7 5.9 %copy-start.45 = (f32[2,10,258]{2,1,0:T(8,128)}, f32[2,10,258]{2,1,0:T(8,128)S(1)}, u32[]{:S(2)}) copy-start(f32[2,10,258]{2,1,0:T(8,128)S(1)} %fusion.526) | copy-start | bytes 61924
  86.6 5.8 %copy-start.47 = (f32[2,8,256]{2,1,0:T(8,128)S(1)}, f32[2,8,256]{2,1,0:T(8,128)}, u32[]{:S(2)}) copy-start(f32[2,8,256]{2,1,0:T(8,128)} %param.18) | copy-start | bytes 49156
  86.6 6.9 %copy-start.61 = (f32[2,256]{1,0:T(2,128)S(1)}, f32[2,256]{1,0:T(2,128)}, u32[]{:S(2)}) copy-start(f32[2,256]{1,0:T(2,128)} %copy-done.60) | copy-start | bytes 6148
  91.1 26.5 %copy-start.10 = (f32[32,10,258]{2,1,0:T(8,128)S(1)}, f32[32,10,258]{2,1,0:T(8,128)}, u32[]{:S(2)}) copy-start(f32[32,10,258]{2,1,0:T(8,128)} %copy-done.9) | copy-start | bytes 990724
  92.4 25.3 %copy-start.1 = (f32[32,10,258]{2,1,0:T(8,128)S(1)}, f32[32,10,258]{2,1,0:T(8,128)}, u32[]{:S(2)}) copy-start(f32[32,10,258]{2,1,0:T(8,128)} %copy-done) | copy-start | bytes 990724
  92.4 25.3 %copy-start.4 = (f32[32,10,258]{2,1,0:T(8,128)S(1)}, f32[32,10,258]{2,1,0:T(8,128)}, u32[]{:S(2)}) copy-start(f32[32,10,258]{2,1,0:T(8,128)} %copy-done.3) | copy-start | bytes 990724
  92.4 25.3 %copy-start.7 = (f32[32,10,258]{2,1,0:T(8,128)S(1)}, f32[32,10,258]{2,1,0:T(8,128)}, u32[]{:S(2)}) copy-start(f32[32,10,258]{2,1,0:T(8,128)} %copy-done.6) | copy-start | bytes 990724
  95.1 53.5 %copy-start.50 = (f32[8,256]{1,0:T(8,128)}, f32[8,256]{1,0:T(8,128)S(1)}, u32[]{:S(2)}) copy-start(f32[8,256]{1,0:T(8,128)S(1)} %get-tuple-element.60) | copy-start | bytes 24580
  95.1 6.1 %collective-permute-start.12 = (f32[2,256]{1,0:T(2,128)S(1)}, f32[2,256]{1,0:T(2,128)S(1)}, u32[]{:S(2)}, u32[]{:S(2)}) collective-permute-start(f32[2,256]{1,0:T(2,128)S(1)} %get-tuple-element.259), channel_id=1, source_target_pairs={{0,16},{16,32},{32,48},{48,64},{64,80},{80,96},{96,112},{1,17},{17... | collective-permute-start | bytes 6152 | tf_op jit(solution)/shard_map/ppermute | solution.py:41
  99.2 4.9 %collective-permute-start.13 = (f32[2,256]{1,0:T(2,128)S(1)}, f32[2,256]{1,0:T(2,128)S(1)}, u32[]{:S(2)}, u32[]{:S(2)}) collective-permute-start(f32[2,256]{1,0:T(2,128)S(1)} %get-tuple-element.260), channel_id=1, source_target_pairs={{16,0},{32,16},{48,32},{64,48},{80,64},{96,80},{112,96},{17,1},{33... | collective-permute-start | bytes 6152 | tf_op jit(solution)/shard_map/ppermute | solution.py:44
  104.1 10.3 %copy-start.65 = (f32[2,256]{1,0:T(2,128)}, f32[2,256]{1,0:T(2,128)S(1)}, u32[]{:S(2)}) copy-start(f32[2,256]{1,0:T(2,128)S(1)} %collective-permute-done.13) | copy-start | bytes 6148
  104.2 6.9 %collective-permute-start.14 = (f32[12,2]{1,0:T(8,128)S(1)}, f32[12,2]{1,0:T(8,128)S(1)}, u32[]{:S(2)}, u32[]{:S(2)}) collective-permute-start(f32[12,2]{1,0:T(8,128)S(1)} %get-tuple-element.250), channel_id=1, source_target_pairs={{0,1},{1,2},{2,3},{3,4},{4,5},{5,6},{6,7},{7,8},{8,9},{9,10},{10,1... | collective-permute-start | bytes 296 | tf_op jit(solution)/shard_map/ppermute | solution.py:41
  109.7 4.7 %collective-permute-start.15 = (f32[12,2]{1,0:T(8,128)S(1)}, f32[12,2]{1,0:T(8,128)S(1)}, u32[]{:S(2)}, u32[]{:S(2)}) collective-permute-start(f32[12,2]{1,0:T(8,128)S(1)} %get-tuple-element.251), channel_id=1, source_target_pairs={{1,0},{2,1},{3,2},{4,3},{5,4},{6,5},{7,6},{8,7},{9,8},{10,9},{11,1... | collective-permute-start | bytes 296 | tf_op jit(solution)/shard_map/ppermute | solution.py:44
  111.2 3.3 %copy-start.56 = (f32[12,2]{1,0:T(8,128)}, f32[12,2]{1,0:T(8,128)S(1)}, u32[]{:S(2)}) copy-start(f32[12,2]{1,0:T(8,128)S(1)} %collective-permute-done.14) | copy-start | bytes 292
  135.0 1.6 copy-start.37
  135.0 1.6 copy-start.39
  135.0 1.6 copy-start.42
  185.9 19.5 %copy-start.2 = (f32[32,10,258]{2,1,0:T(8,128)S(1)}, f32[32,10,258]{2,1,0:T(8,128)}, u32[]{:S(2)}) copy-start(f32[32,10,258]{2,1,0:T(8,128)} %copy-done) | copy-start | bytes 990724
  186.0 19.5 %copy-start.5 = (f32[32,10,258]{2,1,0:T(8,128)S(1)}, f32[32,10,258]{2,1,0:T(8,128)}, u32[]{:S(2)}) copy-start(f32[32,10,258]{2,1,0:T(8,128)} %copy-done.3) | copy-start | bytes 990724
  186.0 19.5 %copy-start.8 = (f32[32,10,258]{2,1,0:T(8,128)S(1)}, f32[32,10,258]{2,1,0:T(8,128)}, u32[]{:S(2)}) copy-start(f32[32,10,258]{2,1,0:T(8,128)} %copy-done.6) | copy-start | bytes 990724
  186.9 15.9 %copy-start.48 = (f32[8,256]{1,0:T(8,128)}, f32[8,256]{1,0:T(8,128)S(1)}, u32[]{:S(2)}) copy-start(f32[8,256]{1,0:T(8,128)S(1)} %fusion.562) | copy-start | bytes 24580
  186.9 7.6 %collective-permute-start.16 = (f32[2,256]{1,0:T(2,128)S(1)}, f32[2,256]{1,0:T(2,128)S(1)}, u32[]{:S(2)}, u32[]{:S(2)}) collective-permute-start(f32[2,256]{1,0:T(2,128)S(1)} %get-tuple-element.257), channel_id=1, source_target_pairs={{0,16},{16,32},{32,48},{48,64},{64,80},{80,96},{96,112},{1,17},{17... | collective-permute-start | bytes 6152 | tf_op jit(solution)/shard_map/ppermute | solution.py:41
  192.0 4.9 %collective-permute-start.17 = (f32[2,256]{1,0:T(2,128)S(1)}, f32[2,256]{1,0:T(2,128)S(1)}, u32[]{:S(2)}, u32[]{:S(2)}) collective-permute-start(f32[2,256]{1,0:T(2,128)S(1)} %get-tuple-element.258), channel_id=1, source_target_pairs={{16,0},{32,16},{48,32},{64,48},{80,64},{96,80},{112,96},{17,1},{33... | collective-permute-start | bytes 6152 | tf_op jit(solution)/shard_map/ppermute | solution.py:44
  194.5 9.1 %copy-start.63 = (f32[2,256]{1,0:T(2,128)}, f32[2,256]{1,0:T(2,128)S(1)}, u32[]{:S(2)}) copy-start(f32[2,256]{1,0:T(2,128)S(1)} %collective-permute-done.16) | copy-start | bytes 6148
  196.9 6.7 %copy-start.64 = (f32[2,256]{1,0:T(2,128)}, f32[2,256]{1,0:T(2,128)S(1)}, u32[]{:S(2)}) copy-start(f32[2,256]{1,0:T(2,128)S(1)} %collective-permute-done.17) | copy-start | bytes 6148
  197.0 2.8 %collective-permute-start.18 = (f32[12,2]{1,0:T(8,128)S(1)}, f32[12,2]{1,0:T(8,128)S(1)}, u32[]{:S(2)}, u32[]{:S(2)}) collective-permute-start(f32[12,2]{1,0:T(8,128)S(1)} %get-tuple-element.248), channel_id=1, source_target_pairs={{0,1},{1,2},{2,3},{3,4},{4,5},{5,6},{6,7},{7,8},{8,9},{9,10},{10,1... | collective-permute-start | bytes 296 | tf_op jit(solution)/shard_map/ppermute | solution.py:41
  198.3 4.4 %collective-permute-start.19 = (f32[12,2]{1,0:T(8,128)S(1)}, f32[12,2]{1,0:T(8,128)S(1)}, u32[]{:S(2)}, u32[]{:S(2)}) collective-permute-start(f32[12,2]{1,0:T(8,128)S(1)} %get-tuple-element.249), channel_id=1, source_target_pairs={{1,0},{2,1},{3,2},{4,3},{5,4},{6,5},{7,6},{8,7},{9,8},{10,9},{11,1... | collective-permute-start | bytes 296 | tf_op jit(solution)/shard_map/ppermute | solution.py:44
  199.8 3.8 %copy-start.54 = (f32[12,2]{1,0:T(8,128)}, f32[12,2]{1,0:T(8,128)S(1)}, u32[]{:S(2)}) copy-start(f32[12,2]{1,0:T(8,128)S(1)} %collective-permute-done.18) | copy-start | bytes 292
  205.5 8.8 %copy-start.11 = (f32[32,10,258]{2,1,0:T(8,128)S(1)}, f32[32,10,258]{2,1,0:T(8,128)}, u32[]{:S(2)}) copy-start(f32[32,10,258]{2,1,0:T(8,128)} %copy-done.9) | copy-start | bytes 990724
  223.0 1.6 copy-start.35
  223.0 1.6 copy-start.40
  223.0 1.6 copy-start.43
  226.3 4.1 %copy-start.27 = (f32[32,8,256]{2,1,0:T(8,128)S(1)}, f32[32,8,256]{2,1,0:T(8,128)}, u32[]{:S(2)}) copy-start(f32[32,8,256]{2,1,0:T(8,128)} %get-tuple-element.72) | copy-start | bytes 786436
  226.3 4.1 %copy-start.28 = (f32[32,8,256]{2,1,0:T(8,128)S(1)}, f32[32,8,256]{2,1,0:T(8,128)}, u32[]{:S(2)}) copy-start(f32[32,8,256]{2,1,0:T(8,128)} %get-tuple-element.73) | copy-start | bytes 786436
  226.3 4.2 %copy-start.29 = (f32[32,8,256]{2,1,0:T(8,128)S(1)}, f32[32,8,256]{2,1,0:T(8,128)}, u32[]{:S(2)}) copy-start(f32[32,8,256]{2,1,0:T(8,128)} %get-tuple-element.74) | copy-start | bytes 786436
  230.4 6.1 %copy-start.49 = (f32[8,256]{1,0:T(8,128)S(1)}, f32[8,256]{1,0:T(8,128)}, u32[]{:S(2)}) copy-start(f32[8,256]{1,0:T(8,128)} %copy-done.48) | copy-start | bytes 24580
  (22 other events, 23.2 us)
where the time goes:
time: 281 us; the launch traced here: 276 us
  other arithmetic  111 us (40%)
  blocking collectives  66.3 us (24%)
  starting transfers between devices  55.6 us (20%)
  waiting for transfers between devices  23.2 us (8%)
  local copies, waits for them, and re-layouts  12.1 us (4%)
  between operations  7.96 us (3%)
    another operation x12, other arithmetic, couple(): return jnp.stack([along_one, along_two])  80.1 us
    psum x8, blocking collectives, by_axis(): value = lax.psum(value, axis)  66.3 us
    ppermute x10, starting transfers between devices, extended(): lax.ppermute(lax.slice_in_dim(block, block.shape[dim] - width, None, axis...  38.5 us
    ppermute x10, waiting for transfers between devices, extended(): lax.ppermute(lax.slice_in_dim(block, 0, width, axis=dim), axis, backward)  19.7 us
    ppermute x10, starting transfers between devices, extended(): lax.ppermute(lax.slice_in_dim(block, 0, width, axis=dim), axis, backward)  17 us
    unnamed x147, local copies, waits for them, and re-layouts  6.45 us
  transfers between devices with their start and end apart: 20, of which 7 were waited for; matrix products, arithmetic and copies ran while one was open for 2% of the time, Pallas kernels for 0%

commit v1 on v0

v1 whole, which is shorter than its diff:
```python
import functools

import jax
import jax.numpy as jnp
from jax import lax
from jax.experimental import pallas as pl
from jax.experimental.pallas import tpu as pltpu
from jax.sharding import PartitionSpec as P

MESH = pl.DeviceIdType.MESH
F32 = jnp.float32

VERT_COUPLING = 128.0
SINK_RATE = 0.0625
BED_DRAG = 0.5
OFFSET_WEIGHT = 0.0019
CROSS_SHARE = 0.5
REG_GAMMA = 0.02
REG_SMOOTH = 1.0
DIAG_SCALE = 0.003

ROWS = 8
LANES = 128
NEIGHBOURS = [(dx, dy) for dx in (-1, 0, 1) for dy in (-1, 0, 1) if (dx, dy) != (0, 0)]
SIDEWAYS = [(dx, dy) for dx in (-1, 0, 1) for dy in (-1, 1)]


def row_roll(tile, shift):
    return pltpu.roll(tile, shift % ROWS, axis=0)


def lane_roll(tile, shift):
    shift = shift % LANES
    return tile if shift == 0 else pltpu.roll(tile, shift, axis=1)


def kernel(
    grad_h, warm_h, eta_h, coef_h, slide_h, weight_h, ice_h, ground_h,
    sol_o, res_o,
    grad_v, warm_v, eta_v, coef_v, slide_v, weight_v, ice_v, ground_v,
    w_v, u_v, inva_v,
    wrow_s, wrow_r, wedge_s, wedge_r,
    frow_s, frow_r, fedge_s, fedge_r,
    krow_s, krow_r, kedge_s, kedge_r,
    suma_s, suma_r, sumb_s, sumb_r,
    in_sem, row_send, row_recv, edge_send, edge_recv, suma_send, suma_recv, sumb_send, sumb_recv,
    *, nx, ny, levels,
):
    mx = lax.axis_index("gx")
    my = lax.axis_index("gy")

    def at(dx, dy):
        return (lax.rem(mx + (dx + nx), nx), lax.rem(my + (dy + ny), ny))

    pairs = [
        (eta_h, eta_v), (coef_h, coef_v), (ground_h, ground_v), (ice_h, ice_v),
        (slide_h, slide_v), (weight_h, weight_v), (grad_h, grad_v), (warm_h, warm_v),
    ]
    loads = [pltpu.make_async_copy(src, dst, in_sem.at[i]) for i, (src, dst) in enumerate(pairs)]
    for load in loads:
        load.start()

    barrier = pltpu.get_barrier_semaphore()
    peers = [at(dx, dy) for dx, dy in NEIGHBOURS]
    peers += [at(k, 0) for k in range(2, nx - 1)]
    peers += [at(0, k) for k in range(2, ny - 1)]
    for peer in peers:
        pl.semaphore_signal(barrier, inc=1, device_id=peer, device_id_type=MESH)

    row_id = lax.broadcasted_iota(jnp.int32, (ROWS, LANES), 0)
    lane_id = lax.broadcasted_iota(jnp.int32, (ROWS, LANES), 1)
    row_first = row_id == 0
    row_last = row_id == ROWS - 1
    lane_first = lane_id == 0
    lane_last = lane_id == LANES - 1
    low_half = lane_id < LANES // 2

    def tiles(value):
        return [value[:, :LANES], value[:, LANES:]]

    for load in loads[:3]:
        load.wait()
    friction = ground_v[...].astype(F32) * coef_v[...]

    slot = lambda z, f: 2 * (levels - 1 - z) + f
    rows_packed = None
    edge_packed = jnp.zeros((ROWS, LANES), F32)
    w = jnp.ones((ROWS, 2 * LANES), F32)
    eta = eta_v[levels - 1]
    flux = SINK_RATE * eta
    for z in range(levels - 1, -1, -1):
        if z < levels - 1:
            above, eta = eta, eta_v[z]
            inva = 1.0 / ((0.5 * VERT_COUPLING) * (above + eta))
            inva_v[z] = inva
            w = w + flux * inva
            flux = flux + (SINK_RATE * eta) * w
        for f, field in enumerate((w, eta * w)):
            m = slot(z, f)
            w_v[m] = field
            r = m % 4
            parts = [row_roll(t, 2 * r) for t in tiles(field)]
            if r == 0:
                rows_packed = parts
            else:
                here = (row_id == 2 * r) | (row_id == 2 * r - 1)
                rows_packed = [jnp.where(here, a, b) for a, b in zip(parts, rows_packed)]
            if r == 3:
                wrow_s[m // 4, :, :LANES] = rows_packed[0]
                wrow_s[m // 4, :, LANES:] = rows_packed[1]
            t0, t1 = tiles(field)
            both = lane_roll(jnp.where(low_half, t0, t1), 2 * m)
            here = (lane_id == 2 * m) | (lane_id == (2 * m - 1) % LANES)
            edge_packed = jnp.where(here, both, edge_packed)
    wedge_s[...] = edge_packed
    total = flux + BED_DRAG * friction * w
    gain = 1.0 / total

    pl.semaphore_wait(barrier, len(peers))

    sends = []

    def send_rows(stage, src, dst):
        out = []
        for k, dx in enumerate((1, -1)):
            copy = pltpu.make_async_remote_copy(
                src_ref=src, dst_ref=dst.at[k],
                send_sem=row_send.at[stage, k], recv_sem=row_recv.at[stage, k],
                device_id=at(dx, 0), device_id_type=MESH,
            )
            copy.start()
            out.append(copy)
        sends.extend(out)
        return out

    def send_edges(stage, src, dst):
        out = []
        for k, (dx, dy) in enumerate(SIDEWAYS):
            copy = pltpu.make_async_remote_copy(
                src_ref=src, dst_ref=dst.at[k],
                send_sem=edge_send.at[stage, k], recv_sem=edge_recv.at[stage, k],
                device_id=at(dx, dy), device_id_type=MESH,
            )
            copy.start()
            out.append(copy)
        sends.extend(out)
        return out

    w_copies = send_edges(0, wedge_s, wedge_r) + send_rows(0, wrow_s, wrow_r)

    for load in loads[3:]:
        load.wait()
    ice = ice_v[...].astype(F32)
    coef = coef_v[...]
    stuck = ice * ground_v[...].astype(F32)
    source_gain = stuck * coef * gain
    fields = [
        source_gain * slide_v[0],
        source_gain * slide_v[1],
        ice * weight_v[...],
        1.0 / (REG_GAMMA * (1.0 + 4.0 * REG_SMOOTH) + DIAG_SCALE * stuck * coef * coef),
        grad_v[...],
        warm_v[...],
    ]

    def pack_edges(values):
        packed = jnp.zeros((ROWS, LANES), F32)
        for f, value in enumerate(values):
            t0, t1 = tiles(value)
            both = lane_roll(jnp.where(low_half, t0, t1), 16 * f)
            group = ((lane_id + 8) % LANES) // 16 == f
            packed = jnp.where(group, both, packed)
        return packed

    for f, value in enumerate(fields):
        frow_s[f] = value
    fedge_s[...] = pack_edges(fields)
    f_copies = send_edges(1, fedge_s, fedge_r) + send_rows(1, frow_s, frow_r)

    u = jnp.ones((ROWS, 2 * LANES), F32)
    flux = SINK_RATE * eta_v[0] + BED_DRAG * friction
    u_v[0] = u
    for z in range(1, levels):
        u = u + flux * inva_v[z - 1]
        flux = flux + (SINK_RATE * eta_v[z]) * u
        u_v[z] = u

    has_up = mx < nx - 1
    has_down = mx > 0
    has_right = my < ny - 1
    has_left = my > 0

    def inside(value, *flags):
        keep = flags[0]
        for flag in flags[1:]:
            keep = keep & flag
        return jnp.where(keep, value, 0.0)

    def join_edges(ref, from_right):
        def got(dx, dy):
            return ref[SIDEWAYS.index((-dx, -dy))]

        own = jnp.where(
            from_right, inside(got(0, 1), has_right), inside(got(0, -1), has_left)
        )
        up = jnp.where(
            from_right, inside(got(1, 1), has_right, has_up), inside(got(1, -1), has_left, has_up)
        )
        down = jnp.where(
            from_right,
            inside(got(-1, 1), has_right, has_down),
            inside(got(-1, -1), has_left, has_down),
        )
        return own, up, down

    for copy in w_copies:
        copy.wait_recv()

    even_lane = lane_id % 2 == 0
    even_row = row_id % 2 == 0
    e_own, e_up, e_down = join_edges(wedge_r, even_lane)
    e_beyond = jnp.where(row_id < 4, e_up, e_down)
    e_plus = row_roll(jnp.where(row_first, e_beyond, e_own), -1)
    e_minus = row_roll(jnp.where(row_last, e_beyond, e_own), 1)
    edge_of = {0: e_own, 1: e_plus, -1: e_minus}

    sums = {n: [None, None] for n in NEIGHBOURS}
    beyond_rows = [None, None]
    for zi in range(levels):
        z = levels - 1 - zi
        eta = eta_v[z]
        u = u_v[z]
        near_u = jnp.zeros_like(u)
        near_eu = jnp.zeros_like(u)
        if z > 0:
            near_u = near_u + u_v[z - 1]
            near_eu = near_eu + u_v[z - 1] * eta_v[z - 1]
        if z < levels - 1:
            near_u = near_u + u_v[z + 1]
            near_eu = near_eu + u_v[z + 1] * eta_v[z + 1]
        eu = eta * u
        straight = (eu + 0.5 * near_eu, u + 0.5 * near_u)
        slanted = (0.5 * eu + (1.0 / 3.0) * near_eu, 0.5 * u + (1.0 / 3.0) * near_u)
        for f in range(2):
            m = slot(z, f)
            g, r = m // 4, m % 4
            if r == 0:
                from_down = inside(wrow_r[0, g], has_down)
                from_up = inside(wrow_r[1, g], has_up)
                beyond_rows = [
                    jnp.where(even_row, a, b) for a, b in zip(tiles(from_up), tiles(from_down))
                ]
            own = tiles(w_v[m])
            beyond = [row_roll(t, -2 * r) for t in beyond_rows]
            by_row = {
                0: own,
                1: [row_roll(jnp.where(row_first, b, t), -1) for b, t in zip(beyond, own)],
                -1: [row_roll(jnp.where(row_last, b, t), 1) for b, t in zip(beyond, own)],
            }
            weights = {1: tiles(straight[f]), 2: tiles(slanted[f])}
            for dx in (-1, 0, 1):
                t0, t1 = by_row[dx]
                edge = lane_roll(edge_of[dx], -2 * m)
                by_lane = {
                    0: [t0, t1],
                    1: [
                        lane_roll(jnp.where(lane_first, t1, t0), -1),
                        lane_roll(jnp.where(lane_first, edge, t1), -1),
                    ],
                    -1: [
                        lane_roll(jnp.where(lane_last, edge, t0), 1),
                        lane_roll(jnp.where(lane_last, t0, t1), 1),
                    ],
                }
                for dy in (-1, 0, 1):
                    if (dx, dy) == (0, 0):
                        continue
                    for j in range(2):
                        term = weights[abs(dx) + abs(dy)][j] * by_lane[dy][j]
                        old = sums[dx, dy][j]
                        sums[dx, dy][j] = term if old is None else old + term
    scaled = [(0.5 * OFFSET_WEIGHT) * t for t in tiles(gain)]
    coefs = []
    for i, n in enumerate(NEIGHBOURS):
        pair = [scaled[j] * sums[n][j] for j in range(2)]
        coefs.append(jnp.concatenate(pair, axis=1))
        krow_s[i, :, :LANES] = pair[0]
        krow_s[i, :, LANES:] = pair[1]
    kedge_s[...] = pack_edges(coefs)
    k_copies = send_edges(2, kedge_s, kedge_r) + send_rows(2, krow_s, krow_r)

    group_right = lane_id % 16 < 8

    def wide(values, row_ref, edge_ref):
        joined = join_edges(edge_ref, group_right)
        out = []
        for f, value in enumerate(values):
            rows = [
                tiles(value),
                tiles(inside(row_ref[1, f], has_up)),
                tiles(inside(row_ref[0, f], has_down)),
            ]
            out.append(
                [rows[i] + [lane_roll(joined[i], -16 * f)] for i in range(3)]
            )
        return out

    for copy in f_copies:
        copy.wait_recv()
    src0, src1, obs, diag, grad, warm = wide(fields, frow_r, fedge_r)

    def each(fn, *args):
        return [[fn(*(a[i][j] for a in args)) for j in range(3)] for i in range(3)]

    def from_row(a, dx):
        if dx == 0:
            return a
        mask = row_first if dx > 0 else row_last
        return [
            [row_roll(jnp.where(mask, a[(i + dx) % 3][j], a[i][j]), -dx) for j in range(3)]
            for i in range(3)
        ]

    def from_lane(a, dy):
        if dy == 0:
            return a
        mask = lane_first if dy > 0 else lane_last
        return [
            [lane_roll(jnp.where(mask, a[i][(j + dy) % 3], a[i][j]), -dy) for j in range(3)]
            for i in range(3)
        ]

    def plus(*args):
        return each(lambda *t: functools.reduce(lambda a, b: a + b, t), *args)

    def times(a, b):
        return each(lambda s, t: s * t, a, b)

    def axpy(factor, a, b):
        return each(lambda s, t: factor * s + t, a, b)

    def smooth(q):
        return each(
            lambda c, a, b, d, e: REG_GAMMA * (c + REG_SMOOTH * (4.0 * c - (a + b + d + e))),
            q, from_row(q, 1), from_row(q, -1), from_lane(q, 1), from_lane(q, -1),
        )

    def to_surface(q):
        spread = [times(src0, q), times(src1, q)]
        result = list(spread)
        for dx in (-1, 0, 1):
            near_row = [from_row(s, dx) for s in spread]
            for dy in (-1, 0, 1):
                if (dx, dy) == (0, 0):
                    continue
                near = [from_lane(s, dy) for s in near_row]
                weight = stencil[NEIGHBOURS.index((dx, dy))]
                for c in range(2):
                    value = near[c]
                    if dx * dy:
                        value = axpy(CROSS_SHARE * dx * dy, near[1 - c], value)
                    result[c] = plus(result[c], times(weight, value))
        return result

    def to_bed(surface):
        traction = [times(obs, s) for s in surface]
        result = list(traction)
        twisted = {
            s: [axpy(CROSS_SHARE * s, traction[1 - c], traction[c]) for c in range(2)]
            for s in (-1, 1)
        }
        for dy in (-1, 0, 1):
            for c in range(2):
                gathered = None
                for dx in (-1, 0, 1):
                    if (dx, dy) == (0, 0):
                        continue
                    value = twisted[dx * dy][c] if dx * dy else traction[c]
                    weight = stencil[NEIGHBOURS.index((-dx, -dy))]
                    term = from_row(times(weight, value), dx)
                    gathered = term if gathered is None else plus(gathered, term)
                result[c] = plus(result[c], from_lane(gathered, dy))
        return plus(times(src0, result[0]), times(src1, result[1]))

    def hessian(q):
        return plus(to_bed(to_surface(q)), smooth(q))

    for copy in k_copies:
        copy.wait_recv()
    stencil = wide(coefs, krow_r, kedge_r)

    resid = each(lambda a, b: a - b, grad, hessian(warm))
    dir0 = times(diag, resid)
    img0 = hessian(dir0)
    dir1 = times(diag, img0)
    surf1 = to_surface(dir1)
    smooth1 = smooth(dir1)

    def own_sum(fn):
        t = fn(0) + fn(1)
        return jnp.sum(t, axis=0, keepdims=True)

    dots = [
        own_sum(lambda j: resid[0][j] * dir0[0][j]),
        own_sum(lambda j: dir0[0][j] * img0[0][j]),
        own_sum(lambda j: img0[0][j] * dir1[0][j]),
        own_sum(
            lambda j: obs[0][j] * (surf1[0][0][j] * surf1[0][0][j] + surf1[1][0][j] * surf1[1][0][j])
            + dir1[0][j] * smooth1[0][j]
        ),
    ]
    partial = jnp.zeros((ROWS, LANES), F32)
    for q, value in enumerate(dots):
        partial = jnp.where(row_id == q, value, partial)

    def exchange(value, stage_ref, recv_ref, send_sems, recv_sems, me, n, device):
        stage_ref[...] = value
        out = []
        for k in range(1, n):
            copy = pltpu.make_async_remote_copy(
                src_ref=stage_ref, dst_ref=recv_ref.at[me],
                send_sem=send_sems.at[k], recv_sem=recv_sems.at[k],
                device_id=device(k), device_id_type=MESH,
            )
            copy.start()
            out.append(copy)
        recv_ref[me] = value
        sends.extend(out)
        return out

    a_copies = exchange(
        partial, suma_s, suma_r, suma_send, suma_recv, mx, nx, lambda k: at(k, 0)
    )
    img1 = plus(to_bed(surf1), smooth1)
    for copy in a_copies:
        copy.wait_recv()
    partial = suma_r[0]
    for k in range(1, nx):
        partial = partial + suma_r[k]
    b_copies = exchange(
        partial, sumb_s, sumb_r, sumb_send, sumb_recv, my, ny, lambda k: at(0, k)
    )
    for copy in b_copies:
        copy.wait_recv()
    partial = sumb_r[0]
    for k in range(1, ny):
        partial = partial + sumb_r[k]
    full = jnp.sum(partial, axis=1, keepdims=True)
    s0, s1, s2, s3 = (jnp.broadcast_to(full[q : q + 1], (ROWS, LANES)) for q in range(4))

    step0 = s0 / s1
    ratio = (step0 * step0 * s2 - s0) / s0
    grow = 1.0 + ratio
    bend = grow * grow * s1 - 2.0 * grow * step0 * s2 + step0 * step0 * s3
    step1 = ratio * s0 / bend
    for j in range(2):
        cols = slice(j * LANES, (j + 1) * LANES)
        along = grow * dir0[0][j] - step0 * dir1[0][j]
        image = grow * img0[0][j] - step0 * img1[0][j]
        sol_o[:, cols] = warm[0][j] + step0 * dir0[0][j] + step1 * along
        res_o[:, cols] = resid[0][j] - step0 * img0[0][j] - step1 * image

    for copy in sends:
        copy.wait_send()


def solution(mesh):
    nx, ny = mesh.shape["gx"], mesh.shape["gy"]

    def on_device(grad, warm, eta, coef, slide, weight, ice, ground):
        levels, rows, cols = eta.shape
        vmem = lambda *shape: pltpu.VMEM(shape, F32)
        wslots = levels // 2
        dma = lambda *shape: pltpu.SemaphoreType.DMA(shape)
        call = pl.pallas_call(
            functools.partial(kernel, nx=nx, ny=ny, levels=levels),
            out_shape=(
                jax.ShapeDtypeStruct((rows, cols), F32),
                jax.ShapeDtypeStruct((rows, cols), F32),
            ),
            in_specs=[pl.BlockSpec(memory_space=pl.ANY)] * 8,
            out_specs=(
                pl.BlockSpec(memory_space=pltpu.VMEM),
                pl.BlockSpec(memory_space=pltpu.VMEM),
            ),
            scratch_shapes=[
                vmem(rows, cols), vmem(rows, cols), vmem(levels, rows, cols), vmem(rows, cols),
                vmem(2, rows, cols), vmem(rows, cols),
                pltpu.VMEM((rows, cols), jnp.int32), pltpu.VMEM((rows, cols), jnp.int32),
                vmem(2 * levels, rows, cols), vmem(levels, rows, cols), vmem(levels, rows, cols),
                vmem(wslots, rows, cols), vmem(2, wslots, rows, cols),
                vmem(rows, LANES), vmem(6, rows, LANES),
                vmem(6, rows, cols), vmem(2, 6, rows, cols),
                vmem(rows, LANES), vmem(6, rows, LANES),
                vmem(8, rows, cols), vmem(2, 8, rows, cols),
                vmem(rows, LANES), vmem(6, rows, LANES),
                vmem(rows, LANES), vmem(nx, rows, LANES),
                vmem(rows, LANES), vmem(ny, rows, LANES),
                dma(8), dma(3, 2), dma(3, 2), dma(3, 6), dma(3, 6),
                dma(nx), dma(nx), dma(ny), dma(ny),
            ],
            compiler_params=pltpu.CompilerParams(collective_id=0, has_side_effects=True),
        )
        return call(grad, warm, eta, coef, slide, weight, ice, ground)

    return jax.shard_map(
        on_device,
        mesh=mesh,
        in_specs=(
            P("gx", "gy"), P("gx", "gy"), P(None, "gx", "gy"), P("gx", "gy"),
            P(None, "gx", "gy"), P("gx", "gy"), P("gx", "gy"), P("gx", "gy"),
        ),
        out_specs=(P("gx", "gy"), P("gx", "gy")),
        check_vma=False,
    )
```

time: 281 us -> 40.5 us (0.14); the launches traced: 276 us -> 40.3 us
  other arithmetic: 111 us -> 0 us
  blocking collectives: 66.3 us -> 0 us
  starting transfers between devices: 55.6 us -> 0 us
  Pallas kernels: 0 us -> 37.8 us
  waiting for transfers between devices: 23.2 us -> 0 us
  local copies, waits for them, and re-layouts: 12.1 us -> 1.9 us
  between operations: 7.96 us -> 0.65 us
    another operation x13 -> x0, other arithmetic: 80.1 us -> none  [the longest x12 80.1 us: couple(): return jnp.stack([along_one, along_two])]
    psum x8 -> x0, blocking collectives: 66.3 us -> none  [by_axis(): value = lax.psum(value, axis)]
    ppermute x20 -> x0, starting transfers between devices: 55.6 us -> none  [the longest x10 38.5 us: extended(): lax.ppermute(lax.slice_in_dim(block, block.shape[dim] - width, None, axis...]
    pallas_call x0 -> x1, Pallas kernels: none -> 37.8 us  [on_device(): return call(grad, warm, eta, coef, slide, weight, ice, ground)]
    ppermute x20 -> x0, waiting for transfers between devices: 23.2 us -> none  [the longest x10 19.7 us: extended(): lax.ppermute(lax.slice_in_dim(block, 0, width, axis=dim), axis, backward)]
    reduce_sum x11 -> x0, other arithmetic: 14.7 us -> none  [the longest x3 4.79 us: hessian(): jnp.sum(top_inner[None] * coupled, axis=1)]
    mul x34 -> x0, other arithmetic: 9.35 us -> none  [the longest x3 2.58 us: hessian(): first_state = bottom_wide[None] * spread[:, None]]
    slice x12 -> x0, local copies, waits for them, and re-layouts: 4.62 us -> none  [the longest x9 2.29 us: extended(): lax.slice_in_dim(block, block.shape[dim] - width, None, axis=dim)]
  transfers between devices with their start and end apart: 20 -> 0, of which waited for: 7 -> 0; matrix products, arithmetic and copies ran while one was open for 2% -> 0% of each run, Pallas kernels for 0% -> 0%
where the time goes in v1:
time: 40.5 us; the launch traced here: 40.3 us
  Pallas kernels  37.8 us (93%)
  local copies, waits for them, and re-layouts  1.9 us (5%)
  between operations  0.65 us (2%)
    pallas_call x1, Pallas kernels, on_device(): return call(grad, warm, eta, coef, slide, weight, ice, ground)  37.8 us
    unnamed x4, local copies, waits for them, and re-layouts  1.9 us

profile of v1, /device:TPU:1, one launch (start us, length us, event | category | flops | bytes accessed | tf_op | source)
XLA Modules:
  0.0 40.3 jit_solution(5690301476454926915)
XLA Ops:
  0.6 37.8 %shard_map.95 = (f32[8,256]{1,0:T(8,128)}, f32[8,256]{1,0:T(8,128)}) custom-call(f32[8,256]{1,0:T(8,128)} %grad_h.1, f32[8,256]{1,0:T(8,128)} %warm_h.1, f32[32,8,256]{2,1,0:T(8,128)} %eta_h.1, f32[8,256]{1,0:T(8,128)} %coef_h.1, f32[2,8,256]{2,1,0:T(8,128)} %slide_h.1, f32[8,256]{1,0:T(8,128)} %weight_h.1, s32[8,256]{1,0:T(8,128)} %ice_h.1, s32[8,256]{1,0:T(8,128)} %ground_h.1), custom_call_target="tpu_custom_call" | custom-call | tf_op jit(solution)/shard_map/pallas_call | solution.py:504
  38.4 0.0 copy-start
  38.4 1.3 %copy.12 = f32[8,256]{1,0:T(8,128)} copy(f32[8,256]{1,0:T(8,128)} %get-tuple-element.4) | data formatting | bytes 16384
  39.7 0.0 copy-done
  39.7 0.6 %copy.13 = f32[8,256]{1,0:T(8,128)} copy(f32[8,256]{1,0:T(8,128)S(1)} %copy-done) | data formatting | bytes 16384
Async XLA Ops:
  38.4 1.3 %copy-start = (f32[8,256]{1,0:T(8,128)S(1)}, f32[8,256]{1,0:T(8,128)}, u32[]{:S(2)}) copy-start(f32[8,256]{1,0:T(8,128)} %get-tuple-element.5) | copy-start | bytes 24580

commit v2 on v1

--- a/solution.py
+++ b/solution.py
@@ -38,7 +38,7 @@
     grad_h, warm_h, eta_h, coef_h, slide_h, weight_h, ice_h, ground_h,
     sol_o, res_o,
     grad_v, warm_v, eta_v, coef_v, slide_v, weight_v, ice_v, ground_v,
-    w_v, u_v, inva_v,
+    w_v, wahead_v, wbehind_v, u_v, inva_v, pack_v,
     wrow_s, wrow_r, wedge_s, wedge_r,
     frow_s, frow_r, fedge_s, fedge_r,
     krow_s, krow_r, kedge_s, kedge_r,
@@ -83,7 +83,22 @@
     friction = ground_v[...].astype(F32) * coef_v[...]
 
     slot = lambda z, f: 2 * (levels - 1 - z) + f
-    rows_packed = None
+
+    def pack_row(packed, value, row, m):
+        parts = [row_roll(t, m % ROWS - row) for t in tiles(value)]
+        if m % ROWS == 0:
+            return parts
+        return [jnp.where(row_id == m % ROWS, a, b) for a, b in zip(parts, packed)]
+
+    def put(ref, index, pair):
+        ref[index + (slice(None), slice(0, LANES))] = pair[0]
+        ref[index + (slice(None), slice(LANES, 2 * LANES))] = pair[1]
+
+    def pack_lanes(packed, both, m):
+        here = (lane_id == 2 * m) | (lane_id == (2 * m - 1) % LANES)
+        return jnp.where(here, lane_roll(both, 2 * m), packed)
+
+    first_rows = last_rows = None
     edge_packed = jnp.zeros((ROWS, LANES), F32)
     w = jnp.ones((ROWS, 2 * LANES), F32)
     eta = eta_v[levels - 1]
@@ -98,20 +113,17 @@
         for f, field in enumerate((w, eta * w)):
             m = slot(z, f)
             w_v[m] = field
-            r = m % 4
-            parts = [row_roll(t, 2 * r) for t in tiles(field)]
-            if r == 0:
-                rows_packed = parts
-            else:
-                here = (row_id == 2 * r) | (row_id == 2 * r - 1)
-                rows_packed = [jnp.where(here, a, b) for a, b in zip(parts, rows_packed)]
-            if r == 3:
-                wrow_s[m // 4, :, :LANES] = rows_packed[0]
-                wrow_s[m // 4, :, LANES:] = rows_packed[1]
+            last_rows = pack_row(last_rows, field, ROWS - 1, m)
+            first_rows = pack_row(first_rows, field, 0, m)
+            if m % ROWS == ROWS - 1:
+                put(wrow_s, (0, m // ROWS), last_rows)
+                put(wrow_s, (1, m // ROWS), first_rows)
             t0, t1 = tiles(field)
-            both = lane_roll(jnp.where(low_half, t0, t1), 2 * m)
-            here = (lane_id == 2 * m) | (lane_id == (2 * m - 1) % LANES)
-            edge_packed = jnp.where(here, both, edge_packed)
+            ahead = lane_roll(t0, -1)
+            behind = lane_roll(t1, 1)
+            wahead_v[m] = ahead
+            wbehind_v[m] = behind
+            edge_packed = pack_lanes(edge_packed, jnp.where(low_half, behind, ahead), m)
     wedge_s[...] = edge_packed
     total = flux + BED_DRAG * friction * w
     gain = 1.0 / total
@@ -120,11 +132,11 @@
 
     sends = []
 
-    def send_rows(stage, src, dst):
+    def send_rows(stage, src, dst, split=False):
         out = []
         for k, dx in enumerate((1, -1)):
             copy = pltpu.make_async_remote_copy(
-                src_ref=src, dst_ref=dst.at[k],
+                src_ref=src.at[k] if split else src, dst_ref=dst.at[k],
                 send_sem=row_send.at[stage, k], recv_sem=row_recv.at[stage, k],
                 device_id=at(dx, 0), device_id_type=MESH,
             )
@@ -146,7 +158,7 @@
         sends.extend(out)
         return out
 
-    w_copies = send_edges(0, wedge_s, wedge_r) + send_rows(0, wrow_s, wrow_r)
+    w_copies = send_edges(0, wedge_s, wedge_r) + send_rows(0, wrow_s, wrow_r, split=True)
 
     for load in loads[3:]:
         load.wait()
@@ -213,72 +225,97 @@
         )
         return own, up, down
 
-    for copy in w_copies:
-        copy.wait_recv()
-
-    even_lane = lane_id % 2 == 0
-    even_row = row_id % 2 == 0
-    e_own, e_up, e_down = join_edges(wedge_r, even_lane)
-    e_beyond = jnp.where(row_id < 4, e_up, e_down)
-    e_plus = row_roll(jnp.where(row_first, e_beyond, e_own), -1)
-    e_minus = row_roll(jnp.where(row_last, e_beyond, e_own), 1)
-    edge_of = {0: e_own, 1: e_plus, -1: e_minus}
-
+    row_packs = {}
+    straight_edge = jnp.zeros((ROWS, LANES), F32)
+    slanted_edge = jnp.zeros((ROWS, LANES), F32)
     sums = {n: [None, None] for n in NEIGHBOURS}
-    beyond_rows = [None, None]
-    for zi in range(levels):
-        z = levels - 1 - zi
-        eta = eta_v[z]
+
+    def add(table, key, j, term):
+        table[key][j] = term if table[key][j] is None else table[key][j] + term
+
+    def seam(ahead0, ahead1, behind0, behind1):
+        return (
+            [jnp.where(lane_last, ahead1, ahead0), ahead1],
+            [behind0, jnp.where(lane_first, behind0, behind1)],
+        )
+
+    for z in range(levels - 1, -1, -1):
         u = u_v[z]
-        near_u = jnp.zeros_like(u)
-        near_eu = jnp.zeros_like(u)
-        if z > 0:
-            near_u = near_u + u_v[z - 1]
-            near_eu = near_eu + u_v[z - 1] * eta_v[z - 1]
-        if z < levels - 1:
-            near_u = near_u + u_v[z + 1]
-            near_eu = near_eu + u_v[z + 1] * eta_v[z + 1]
-        eu = eta * u
+        eu = eta_v[z] * u
+        near_u = near_eu = None
+        for other in (z - 1, z + 1):
+            if 0 <= other < levels:
+                beside = u_v[other]
+                near_u = beside if near_u is None else near_u + beside
+                beside = eta_v[other] * beside
+                near_eu = beside if near_eu is None else near_eu + beside
         straight = (eu + 0.5 * near_eu, u + 0.5 * near_u)
         slanted = (0.5 * eu + (1.0 / 3.0) * near_eu, 0.5 * u + (1.0 / 3.0) * near_u)
         for f in range(2):
             m = slot(z, f)
-            g, r = m // 4, m % 4
-            if r == 0:
-                from_down = inside(wrow_r[0, g], has_down)
-                from_up = inside(wrow_r[1, g], has_up)
-                beyond_rows = [
-                    jnp.where(even_row, a, b) for a, b in zip(tiles(from_up), tiles(from_down))
-                ]
-            own = tiles(w_v[m])
-            beyond = [row_roll(t, -2 * r) for t in beyond_rows]
-            by_row = {
-                0: own,
-                1: [row_roll(jnp.where(row_first, b, t), -1) for b, t in zip(beyond, own)],
-                -1: [row_roll(jnp.where(row_last, b, t), 1) for b, t in zip(beyond, own)],
-            }
-            weights = {1: tiles(straight[f]), 2: tiles(slanted[f])}
-            for dx in (-1, 0, 1):
-                t0, t1 = by_row[dx]
-                edge = lane_roll(edge_of[dx], -2 * m)
-                by_lane = {
-                    0: [t0, t1],
-                    1: [
-                        lane_roll(jnp.where(lane_first, t1, t0), -1),
-                        lane_roll(jnp.where(lane_first, edge, t1), -1),
-                    ],
-                    -1: [
-                        lane_roll(jnp.where(lane_last, edge, t0), 1),
-                        lane_roll(jnp.where(lane_last, t0, t1), 1),
-                    ],
-                }
-                for dy in (-1, 0, 1):
-                    if (dx, dy) == (0, 0):
-                        continue
-                    for j in range(2):
-                        term = weights[abs(dx) + abs(dy)][j] * by_lane[dy][j]
-                        old = sums[dx, dy][j]
-                        sums[dx, dy][j] = term if old is None else old + term
+            for kind, value in enumerate((straight[f], slanted[f])):
+                for side, row in enumerate((0, ROWS - 1)):
+                    packed = pack_row(row_packs.get((kind, side)), value, row, m)
+                    row_packs[kind, side] = packed
+                    if m % ROWS == ROWS - 1:
+                        put(pack_v, (kind, side, m // ROWS), packed)
+            s_pair, d_pair = tiles(straight[f]), tiles(slanted[f])
+            straight_edge = pack_lanes(straight_edge, jnp.where(low_half, *s_pair), m)
+            slanted_edge = pack_lanes(slanted_edge, jnp.where(low_half, *d_pair), m)
+            t0, t1 = tiles(w_v[m])
+            plus_pair, minus_pair = seam(wahead_v[m], lane_roll(t1, -1), lane_roll(t0, 1), wbehind_v[m])
+            by_lane = {0: [t0, t1], 1: plus_pair, -1: minus_pair}
+            for j in range(2):
+                for dy in (-1, 1):
+                    add(sums, (0, dy), j, s_pair[j] * by_lane[dy][j])
+                for dx in (-1, 1):
+                    s_rolled = row_roll(s_pair[j], dx)
+                    d_rolled = row_roll(d_pair[j], dx)
+                    for dy in (-1, 0, 1):
+                        rolled = d_rolled if dy else s_rolled
+                        add(sums, (dx, dy), j, rolled * by_lane[dy][j])
+
+    for copy in w_copies:
+        copy.wait_recv()
+
+    even_lane = lane_id % 2 == 0
+    e_own, e_up, e_down = join_edges(wedge_r, ~even_lane)
+    e_beyond = jnp.where(row_id < 4, e_up, e_down)
+    edge_of = {
+        0: e_own,
+        1: row_roll(jnp.where(row_first, e_beyond, e_own), -1),
+        -1: row_roll(jnp.where(row_last, e_beyond, e_own), 1),
+    }
+    edge_sums = {}
+    for dx in (-1, 0, 1):
+        product = (slanted_edge if dx else straight_edge) * edge_of[dx]
+        for dy in (-1, 1):
+            part = jnp.where(even_lane == (dy < 0), product, 0.0)
+            edge_sums[dx, dy] = jnp.sum(part, axis=1, keepdims=True)
+
+    row_sums = {(dx, dy): [None, None] for dx in (-1, 1) for dy in (-1, 0, 1)}
+    for side, flag in ((0, has_down), (1, has_up)):
+        dx = 2 * side - 1
+        for g in range(2 * levels // ROWS):
+            t0, t1 = tiles(inside(wrow_r[side, g], flag))
+            plus_pair, minus_pair = seam(
+                lane_roll(t0, -1), lane_roll(t1, -1), lane_roll(t0, 1), lane_roll(t1, 1)
+            )
+            by_lane = {0: [t0, t1], 1: plus_pair, -1: minus_pair}
+            for dy in (-1, 0, 1):
+                weight = tiles(pack_v[1 if dy else 0, side, g])
+                for j in range(2):
+                    add(row_sums, (dx, dy), j, weight[j] * by_lane[dy][j])
+
+    for (dx, dy), pair in sums.items():
+        for j in range(2):
+            value = pair[j]
+            if dx:
+                beyond = jnp.sum(row_sums[dx, dy][j], axis=0, keepdims=True)
+                value = jnp.where(row_last if dx > 0 else row_first, beyond, row_roll(value, -dx))
+            if dy and j == (dy + 1) // 2:
+                value = jnp.where(lane_last if dy > 0 else lane_first, edge_sums[dx, dy], value)
+            pair[j] = value
     scaled = [(0.5 * OFFSET_WEIGHT) * t for t in tiles(gain)]
     coefs = []
     for i, n in enumerate(NEIGHBOURS):
@@ -470,7 +507,7 @@
     def on_device(grad, warm, eta, coef, slide, weight, ice, ground):
         levels, rows, cols = eta.shape
         vmem = lambda *shape: pltpu.VMEM(shape, F32)
-        wslots = levels // 2
+        wtiles = 2 * levels // ROWS
         dma = lambda *shape: pltpu.SemaphoreType.DMA(shape)
         call = pl.pallas_call(
             functools.partial(kernel, nx=nx, ny=ny, levels=levels),
@@ -487,8 +524,9 @@
                 vmem(rows, cols), vmem(rows, cols), vmem(levels, rows, cols), vmem(rows, cols),
                 vmem(2, rows, cols), vmem(rows, cols),
                 pltpu.VMEM((rows, cols), jnp.int32), pltpu.VMEM((rows, cols), jnp.int32),
-                vmem(2 * levels, rows, cols), vmem(levels, rows, cols), vmem(levels, rows, cols),
-                vmem(wslots, rows, cols), vmem(2, wslots, rows, cols),
+                vmem(2 * levels, rows, cols), vmem(2 * levels, rows, LANES), vmem(2 * levels, rows, LANES),
+                vmem(levels, rows, cols), vmem(levels, rows, cols), vmem(2, 2, wtiles, rows, cols),
+                vmem(2, wtiles, rows, cols), vmem(2, wtiles, rows, cols),
                 vmem(rows, LANES), vmem(6, rows, LANES),
                 vmem(6, rows, cols), vmem(2, 6, rows, cols),
                 vmem(rows, LANES), vmem(6, rows, LANES),

time: 40.5 us -> 29.6 us (0.73)
  Pallas kernels: 37.8 us -> 26.9 us
    pallas_call x1, Pallas kernels: 37.8 us -> 26.9 us  [on_device(): return call(grad, warm, eta, coef, slide, weight, ice, ground)]
where the time goes in v2:
time: 29.6 us; the launch traced here: 29.4 us
  Pallas kernels  26.9 us (91%)
  local copies, waits for them, and re-layouts  1.9 us (6%)
  between operations  0.65 us (2%)
    pallas_call x1, Pallas kernels, on_device(): return call(grad, warm, eta, coef, slide, weight, ice, ground)  26.9 us
    unnamed x4, local copies, waits for them, and re-layouts  1.9 us

profile of v2, /device:TPU:1, one launch (start us, length us, event | category | flops | bytes accessed | tf_op | source)
XLA Modules:
  0.0 29.4 jit_solution(8268470958230732206)
XLA Ops:
  0.6 26.9 %shard_map.95 = (f32[8,256]{1,0:T(8,128)}, f32[8,256]{1,0:T(8,128)}) custom-call(f32[8,256]{1,0:T(8,128)} %grad_h.1, f32[8,256]{1,0:T(8,128)} %warm_h.1, f32[32,8,256]{2,1,0:T(8,128)} %eta_h.1, f32[8,256]{1,0:T(8,128)} %coef_h.1, f32[2,8,256]{2,1,0:T(8,128)} %slide_h.1, f32[8,256]{1,0:T(8,128)} %weight_h.1, s32[8,256]{1,0:T(8,128)} %ice_h.1, s32[8,256]{1,0:T(8,128)} %ground_h.1), custom_call_target="tpu_custom_call" | custom-call | tf_op jit(solution)/shard_map/pallas_call | solution.py:542
  27.5 0.0 copy-start
  27.5 1.3 %copy.12 = f32[8,256]{1,0:T(8,128)} copy(f32[8,256]{1,0:T(8,128)} %get-tuple-element.4) | data formatting | bytes 16384
  28.8 0.0 copy-done
  28.8 0.6 %copy.13 = f32[8,256]{1,0:T(8,128)} copy(f32[8,256]{1,0:T(8,128)S(1)} %copy-done) | data formatting | bytes 16384
Async XLA Ops:
  27.5 1.3 %copy-start = (f32[8,256]{1,0:T(8,128)S(1)}, f32[8,256]{1,0:T(8,128)}, u32[]{:S(2)}) copy-start(f32[8,256]{1,0:T(8,128)} %get-tuple-element.5) | copy-start | bytes 24580

commit v3 on v2

--- a/solution.py
+++ b/solution.py
@@ -22,6 +22,7 @@
 ROWS = 8
 LANES = 128
 NEIGHBOURS = [(dx, dy) for dx in (-1, 0, 1) for dy in (-1, 0, 1) if (dx, dy) != (0, 0)]
+CORNERS_FIRST = sorted(NEIGHBOURS, key=lambda n: -abs(n[0]) - abs(n[1]))
 SIDEWAYS = [(dx, dy) for dx in (-1, 0, 1) for dy in (-1, 1)]
 
 
@@ -36,21 +37,42 @@
 
 def kernel(
     grad_h, warm_h, eta_h, coef_h, slide_h, weight_h, ice_h, ground_h,
-    sol_o, res_o,
+    sol_o, res_o, step_o, along_o, image_o,
     grad_v, warm_v, eta_v, coef_v, slide_v, weight_v, ice_v, ground_v,
     w_v, wahead_v, wbehind_v, u_v, inva_v, pack_v,
     wrow_s, wrow_r, wedge_s, wedge_r,
     frow_s, frow_r, fedge_s, fedge_r,
     krow_s, krow_r, kedge_s, kedge_r,
     suma_s, suma_r, sumb_s, sumb_r,
-    in_sem, row_send, row_recv, edge_send, edge_recv, suma_send, suma_recv, sumb_send, sumb_recv,
+    in_sem, row_send, row_recv, edge_send, edge_recv, known_sem, suma_send, suma_recv, sumb_send, sumb_recv,
     *, nx, ny, levels,
 ):
     mx = lax.axis_index("gx")
     my = lax.axis_index("gy")
 
     def at(dx, dy):
-        return (lax.rem(mx + (dx + nx), nx), lax.rem(my + (dy + ny), ny))
+        return (mx + dx, my + dy)
+
+    def exists(dx, dy):
+        tests = []
+        if dx:
+            tests.append(mx < nx - dx if dx > 0 else mx >= -dx)
+        if dy:
+            tests.append(my < ny - dy if dy > 0 else my >= -dy)
+        return functools.reduce(lambda a, b: a & b, tests)
+
+    def when(flag, *actions):
+        @pl.when(flag)
+        def _():
+            for action in actions:
+                action()
+
+    def signal(sem, peer):
+        pl.semaphore_signal(sem, inc=1, device_id=peer, device_id_type=MESH)
+
+    barrier = pltpu.get_barrier_semaphore()
+    for n in CORNERS_FIRST:
+        when(exists(*n), functools.partial(signal, barrier, at(*n)))
 
     pairs = [
         (eta_h, eta_v), (coef_h, coef_v), (ground_h, ground_v), (ice_h, ice_v),
@@ -59,13 +81,6 @@
     loads = [pltpu.make_async_copy(src, dst, in_sem.at[i]) for i, (src, dst) in enumerate(pairs)]
     for load in loads:
         load.start()
-
-    barrier = pltpu.get_barrier_semaphore()
-    peers = [at(dx, dy) for dx, dy in NEIGHBOURS]
-    peers += [at(k, 0) for k in range(2, nx - 1)]
-    peers += [at(0, k) for k in range(2, ny - 1)]
-    for peer in peers:
-        pl.semaphore_signal(barrier, inc=1, device_id=peer, device_id_type=MESH)
 
     row_id = lax.broadcasted_iota(jnp.int32, (ROWS, LANES), 0)
     lane_id = lax.broadcasted_iota(jnp.int32, (ROWS, LANES), 1)
@@ -128,37 +143,40 @@
     total = flux + BED_DRAG * friction * w
     gain = 1.0 / total
 
-    pl.semaphore_wait(barrier, len(peers))
-
-    sends = []
-
-    def send_rows(stage, src, dst, split=False):
+    def count(*offsets):
+        return 1 + sum(jnp.where(exists(*n), 1, 0) for n in offsets)
+
+    pl.semaphore_wait(barrier, count((1, 0), (-1, 0)) * count((0, 1), (0, -1)) - 1)
+
+    ends = []
+
+    def send(*copies):
+        for (dx, dy), copy in copies:
+            when(exists(dx, dy), copy.start)
+            ends.append((exists(dx, dy), copy))
+        return copies
+
+    def arrive(copies):
+        for (dx, dy), copy in copies:
+            when(exists(-dx, -dy), copy.wait_recv)
+
+    def exchange_edges(stage, edge, edge_in, row_of, rows_in):
         out = []
+        for k, n in enumerate(SIDEWAYS):
+            out.append((n, pltpu.make_async_remote_copy(
+                src_ref=edge, dst_ref=edge_in.at[k],
+                send_sem=edge_send.at[stage, k], recv_sem=edge_recv.at[stage, k],
+                device_id=at(*n), device_id_type=MESH,
+            )))
         for k, dx in enumerate((1, -1)):
-            copy = pltpu.make_async_remote_copy(
-                src_ref=src.at[k] if split else src, dst_ref=dst.at[k],
+            out.append(((dx, 0), pltpu.make_async_remote_copy(
+                src_ref=row_of(k), dst_ref=rows_in.at[k],
                 send_sem=row_send.at[stage, k], recv_sem=row_recv.at[stage, k],
                 device_id=at(dx, 0), device_id_type=MESH,
-            )
-            copy.start()
-            out.append(copy)
-        sends.extend(out)
-        return out
-
-    def send_edges(stage, src, dst):
-        out = []
-        for k, (dx, dy) in enumerate(SIDEWAYS):
-            copy = pltpu.make_async_remote_copy(
-                src_ref=src, dst_ref=dst.at[k],
-                send_sem=edge_send.at[stage, k], recv_sem=edge_recv.at[stage, k],
-                device_id=at(dx, dy), device_id_type=MESH,
-            )
-            copy.start()
-            out.append(copy)
-        sends.extend(out)
-        return out
-
-    w_copies = send_edges(0, wedge_s, wedge_r) + send_rows(0, wrow_s, wrow_r, split=True)
+            )))
+        return send(*out)
+
+    w_copies = exchange_edges(0, wedge_s, wedge_r, lambda k: wrow_s.at[k], wrow_r)
 
     for load in loads[3:]:
         load.wait()
@@ -187,7 +205,7 @@
     for f, value in enumerate(fields):
         frow_s[f] = value
     fedge_s[...] = pack_edges(fields)
-    f_copies = send_edges(1, fedge_s, fedge_r) + send_rows(1, frow_s, frow_r)
+    f_copies = exchange_edges(1, fedge_s, fedge_r, lambda k: frow_s, frow_r)
 
     u = jnp.ones((ROWS, 2 * LANES), F32)
     flux = SINK_RATE * eta_v[0] + BED_DRAG * friction
@@ -197,10 +215,8 @@
         flux = flux + (SINK_RATE * eta_v[z]) * u
         u_v[z] = u
 
-    has_up = mx < nx - 1
-    has_down = mx > 0
-    has_right = my < ny - 1
-    has_left = my > 0
+    has_up, has_down = exists(1, 0), exists(-1, 0)
+    has_right, has_left = exists(0, 1), exists(0, -1)
 
     def inside(value, *flags):
         keep = flags[0]
@@ -275,8 +291,19 @@
                         rolled = d_rolled if dy else s_rolled
                         add(sums, (dx, dy), j, rolled * by_lane[dy][j])
 
-    for copy in w_copies:
-        copy.wait_recv()
+    arrive(w_copies)
+
+    def greet(round, reach):
+        for k, n in enumerate(((reach, 0), (-reach, 0), (0, reach), (0, -reach))):
+            if abs(n[0]) < nx and abs(n[1]) < ny:
+                when(exists(*n), functools.partial(signal, known_sem.at[round, k], at(*n)))
+
+    def greeted(round, reach):
+        for k, n in enumerate(((-reach, 0), (reach, 0), (0, -reach), (0, reach))):
+            if abs(n[0]) < nx and abs(n[1]) < ny:
+                when(exists(*n), functools.partial(pl.semaphore_wait, known_sem.at[round, k], 1))
+
+    greet(0, 2)
 
     even_lane = lane_id % 2 == 0
     e_own, e_up, e_down = join_edges(wedge_r, ~even_lane)
@@ -324,7 +351,7 @@
         krow_s[i, :, :LANES] = pair[0]
         krow_s[i, :, LANES:] = pair[1]
     kedge_s[...] = pack_edges(coefs)
-    k_copies = send_edges(2, kedge_s, kedge_r) + send_rows(2, krow_s, krow_r)
+    k_copies = exchange_edges(2, kedge_s, kedge_r, lambda k: krow_s, krow_r)
 
     group_right = lane_id % 16 < 8
 
@@ -342,8 +369,7 @@
             )
         return out
 
-    for copy in f_copies:
-        copy.wait_recv()
+    arrive(f_copies)
     src0, src1, obs, diag, grad, warm = wide(fields, frow_r, fedge_r)
 
     def each(fn, *args):
@@ -422,8 +448,11 @@
     def hessian(q):
         return plus(to_bed(to_surface(q)), smooth(q))
 
-    for copy in k_copies:
-        copy.wait_recv()
+    greeted(0, 2)
+    greet(1, 4)
+    greeted(1, 4)
+    greet(2, 8)
+    arrive(k_copies)
     stencil = wide(coefs, krow_r, kedge_r)
 
     resid = each(lambda a, b: a - b, grad, hessian(warm))
@@ -461,12 +490,12 @@
             )
             copy.start()
             out.append(copy)
+            ends.append((None, copy))
         recv_ref[me] = value
-        sends.extend(out)
         return out
 
     a_copies = exchange(
-        partial, suma_s, suma_r, suma_send, suma_recv, mx, nx, lambda k: at(k, 0)
+        partial, suma_s, suma_r, suma_send, suma_recv, mx, nx, lambda k: (lax.rem(mx + k, nx), my)
     )
     img1 = plus(to_bed(surf1), smooth1)
     for copy in a_copies:
@@ -474,8 +503,9 @@
     partial = suma_r[0]
     for k in range(1, nx):
         partial = partial + suma_r[k]
+    greeted(2, 8)
     b_copies = exchange(
-        partial, sumb_s, sumb_r, sumb_send, sumb_recv, my, ny, lambda k: at(0, k)
+        partial, sumb_s, sumb_r, sumb_send, sumb_recv, my, ny, lambda k: (mx, lax.rem(my + k, ny))
     )
     for copy in b_copies:
         copy.wait_recv()
@@ -492,13 +522,17 @@
     step1 = ratio * s0 / bend
     for j in range(2):
         cols = slice(j * LANES, (j + 1) * LANES)
-        along = grow * dir0[0][j] - step0 * dir1[0][j]
-        image = grow * img0[0][j] - step0 * img1[0][j]
-        sol_o[:, cols] = warm[0][j] + step0 * dir0[0][j] + step1 * along
-        res_o[:, cols] = resid[0][j] - step0 * img0[0][j] - step1 * image
-
-    for copy in sends:
-        copy.wait_send()
+        sol_o[:, cols] = warm[0][j] + step0 * dir0[0][j]
+        res_o[:, cols] = resid[0][j] - step0 * img0[0][j]
+        step_o[:, cols] = step1
+        along_o[:, cols] = grow * dir0[0][j] - step0 * dir1[0][j]
+        image_o[:, cols] = grow * img0[0][j] - step0 * img1[0][j]
+
+    for flag, copy in ends:
+        if flag is None:
+            copy.wait_send()
+        else:
+            when(flag, copy.wait_send)
 
 
 def solution(mesh):
@@ -511,15 +545,9 @@
         dma = lambda *shape: pltpu.SemaphoreType.DMA(shape)
         call = pl.pallas_call(
             functools.partial(kernel, nx=nx, ny=ny, levels=levels),
-            out_shape=(
-                jax.ShapeDtypeStruct((rows, cols), F32),
-                jax.ShapeDtypeStruct((rows, cols), F32),
-            ),
+            out_shape=(pltpu.VMEM((rows, cols), F32),) * 5,
             in_specs=[pl.BlockSpec(memory_space=pl.ANY)] * 8,
-            out_specs=(
-                pl.BlockSpec(memory_space=pltpu.VMEM),
-                pl.BlockSpec(memory_space=pltpu.VMEM),
-            ),
+            out_specs=(pl.BlockSpec(memory_space=pltpu.VMEM),) * 5,
             scratch_shapes=[
                 vmem(rows, cols), vmem(rows, cols), vmem(levels, rows, cols), vmem(rows, cols),
                 vmem(2, rows, cols), vmem(rows, cols),
@@ -535,11 +563,13 @@
                 vmem(rows, LANES), vmem(nx, rows, LANES),
                 vmem(rows, LANES), vmem(ny, rows, LANES),
                 dma(8), dma(3, 2), dma(3, 2), dma(3, 6), dma(3, 6),
+                pltpu.SemaphoreType.REGULAR((3, 4)),
                 dma(nx), dma(nx), dma(ny), dma(ny),
             ],
             compiler_params=pltpu.CompilerParams(collective_id=0, has_side_effects=True),
         )
-        return call(grad, warm, eta, coef, slide, weight, ice, ground)
+        sol, res, step, along, image = call(grad, warm, eta, coef, slide, weight, ice, ground)
+        return sol + step * along, res - step * image
 
     return jax.shard_map(
         on_device,

time: 29.6 us -> 26.1 us (0.88)
  Pallas kernels: 26.9 us -> 24.8 us
  local copies, waits for them, and re-layouts: 1.9 us -> 0 us
  other arithmetic: 0 us -> 0.61 us
    pallas_call x1, Pallas kernels: 26.9 us -> 24.8 us  [on_device(): call(grad, warm, eta, coef, slide, weight, ice, ground)]
    unnamed x4 -> x0, local copies, waits for them, and re-layouts: 1.9 us -> none
    sub x0 -> x1, other arithmetic: none -> 0.61 us  [on_device(): return (sol + step * along, res - step * image)]
where the time goes in v3:
time: 26.1 us; the launch traced here: 26 us
  Pallas kernels  24.8 us (95%)
  between operations  0.64 us (2%)
  other arithmetic  0.61 us (2%)
    pallas_call x1, Pallas kernels, on_device(): call(grad, warm, eta, coef, slide, weight, ice, ground)  24.8 us
    sub x1, other arithmetic, on_device(): return (sol + step * along, res - step * image)  0.61 us

profile of v3, /device:TPU:1, one launch (start us, length us, event | category | flops | bytes accessed | tf_op | source)
XLA Modules:
  0.0 26.0 jit_solution(15167221469024236486)
XLA Ops:
  0.6 24.8 %shard_map.95 = (f32[8,256]{1,0:T(8,128)S(1)}, f32[8,256]{1,0:T(8,128)S(1)}, f32[8,256]{1,0:T(8,128)S(1)}, f32[8,256]{1,0:T(8,128)S(1)}, f32[8,256]{1,0:T(8,128)S(1)}) custom-call(f32[8,256]{1,0:T(8,128)} %grad_h.1, f32[8,256]{1,0:T(8,128)} %warm_h.1, f32[32,8,256]{2,1,0:T(8,128)} %eta_h.1, f32[8,256]{1,0:T(8,128)} %coef_h.1, f32[2,8,256]{2,1,0:T(8,128)} %slide_h.1, ...), custom_call_target="tpu_custom_call" | custom-call | tf_op jit(solution)/shard_map/pallas_call | solution.py:571
  25.4 0.6 %multiply_subtract_fusion = (f32[8,256]{1,0:T(8,128)}, f32[8,256]{1,0:T(8,128)}) fusion(f32[8,256]{1,0:T(8,128)S(1)} %get-tuple-element.10, f32[8,256]{1,0:T(8,128)S(1)} %get-tuple-element.8, f32[8,256]{1,0:T(8,128)S(1)} %get-tuple-element.11, f32[8,256]{1,0:T(8,128)S(1)} %get-tuple-element.7, f32[8,256]{1,0:T(8,128)S(1)} %get-tuple-element.9), kind=kLoop, calls=%fused_computation | loop fusion | flops 8192 | bytes 57344 | tf_op jit(solution)/shard_map/sub | solution.py:572

commit v4 on v3

--- a/solution.py
+++ b/solution.py
@@ -1,3 +1,4 @@
+import collections
 import functools
 
 import jax
@@ -24,6 +25,8 @@
 NEIGHBOURS = [(dx, dy) for dx in (-1, 0, 1) for dy in (-1, 0, 1) if (dx, dy) != (0, 0)]
 CORNERS_FIRST = sorted(NEIGHBOURS, key=lambda n: -abs(n[0]) - abs(n[1]))
 SIDEWAYS = [(dx, dy) for dx in (-1, 0, 1) for dy in (-1, 1)]
+
+Operator = collections.namedtuple("Operator", "source half_obs stencil")
 
 
 def row_roll(tile, shift):
@@ -185,9 +188,9 @@
     stuck = ice * ground_v[...].astype(F32)
     source_gain = stuck * coef * gain
     fields = [
-        source_gain * slide_v[0],
-        source_gain * slide_v[1],
-        ice * weight_v[...],
+        source_gain * (slide_v[0] + slide_v[1]),
+        source_gain * (slide_v[0] - slide_v[1]),
+        0.5 * ice * weight_v[...],
         1.0 / (REG_GAMMA * (1.0 + 4.0 * REG_SMOOTH) + DIAG_SCALE * stuck * coef * coef),
         grad_v[...],
         warm_v[...],
@@ -370,18 +373,18 @@
         return out
 
     arrive(f_copies)
-    src0, src1, obs, diag, grad, warm = wide(fields, frow_r, fedge_r)
+    *source, half_obs, diag, grad, warm = wide(fields, frow_r, fedge_r)
 
     def each(fn, *args):
-        return [[fn(*(a[i][j] for a in args)) for j in range(3)] for i in range(3)]
+        return [[fn(*(a[i][j] for a in args)) for j in range(3)] for i in range(len(args[0]))]
 
     def from_row(a, dx):
         if dx == 0:
             return a
         mask = row_first if dx > 0 else row_last
         return [
-            [row_roll(jnp.where(mask, a[(i + dx) % 3][j], a[i][j]), -dx) for j in range(3)]
-            for i in range(3)
+            [row_roll(jnp.where(mask, a[(i + dx) % len(a)][j], a[i][j]), -dx) for j in range(3)]
+            for i in range(len(a))
         ]
 
     def from_lane(a, dy):
@@ -390,7 +393,7 @@
         mask = lane_first if dy > 0 else lane_last
         return [
             [lane_roll(jnp.where(mask, a[i][(j + dy) % 3], a[i][j]), -dy) for j in range(3)]
-            for i in range(3)
+            for i in range(len(a))
         ]
 
     def plus(*args):
@@ -398,9 +401,6 @@
 
     def times(a, b):
         return each(lambda s, t: s * t, a, b)
-
-    def axpy(factor, a, b):
-        return each(lambda s, t: factor * s + t, a, b)
 
     def smooth(q):
         return each(
@@ -408,58 +408,62 @@
             q, from_row(q, 1), from_row(q, -1), from_lane(q, 1), from_lane(q, -1),
         )
 
-    def to_surface(q):
-        spread = [times(src0, q), times(src1, q)]
-        result = list(spread)
-        for dx in (-1, 0, 1):
-            near_row = [from_row(s, dx) for s in spread]
+    def to_surface(op, q):
+        out = []
+        for c in range(2):
+            spread = times(op.source[c], q)
+            result = spread
             for dy in (-1, 0, 1):
-                if (dx, dy) == (0, 0):
-                    continue
-                near = [from_lane(s, dy) for s in near_row]
-                weight = stencil[NEIGHBOURS.index((dx, dy))]
-                for c in range(2):
-                    value = near[c]
-                    if dx * dy:
-                        value = axpy(CROSS_SHARE * dx * dy, near[1 - c], value)
-                    result[c] = plus(result[c], times(weight, value))
-        return result
-
-    def to_bed(surface):
-        traction = [times(obs, s) for s in surface]
-        result = list(traction)
-        twisted = {
-            s: [axpy(CROSS_SHARE * s, traction[1 - c], traction[c]) for c in range(2)]
-            for s in (-1, 1)
-        }
-        for dy in (-1, 0, 1):
-            for c in range(2):
+                near_lane = from_lane(spread, dy)
+                for dx in (-1, 0, 1):
+                    if (dx, dy) != (0, 0):
+                        result = plus(result, times(op.stencil[c][dx, dy], from_row(near_lane, dx)))
+            out.append(result)
+        return out
+
+    def to_bed(op, surface):
+        out = []
+        for c in range(2):
+            traction = times(op.half_obs, surface[c])
+            result = traction
+            for dy in (-1, 0, 1):
                 gathered = None
                 for dx in (-1, 0, 1):
-                    if (dx, dy) == (0, 0):
-                        continue
-                    value = twisted[dx * dy][c] if dx * dy else traction[c]
-                    weight = stencil[NEIGHBOURS.index((-dx, -dy))]
-                    term = from_row(times(weight, value), dx)
-                    gathered = term if gathered is None else plus(gathered, term)
-                result[c] = plus(result[c], from_lane(gathered, dy))
-        return plus(times(src0, result[0]), times(src1, result[1]))
-
-    def hessian(q):
-        return plus(to_bed(to_surface(q)), smooth(q))
+                    if (dx, dy) != (0, 0):
+                        term = from_row(times(op.stencil[c][-dx, -dy], traction), dx)
+                        gathered = term if gathered is None else plus(gathered, term)
+                result = plus(result, from_lane(gathered, dy))
+            out.append(times(op.source[c], result))
+        return plus(*out)
+
+    def hessian(op, q):
+        return plus(to_bed(op, to_surface(op, q)), smooth(q))
+
+    def operator(source, half_obs, coefs):
+        return Operator(source, half_obs, [
+            {
+                (dx, dy): each(lambda t: (1.0 + sign * CROSS_SHARE * dx * dy) * t, value) if dx * dy else value
+                for (dx, dy), value in coefs.items()
+            }
+            for sign in (1, -1)
+        ])
+
+    def narrow(a):
+        return [a[0], [jnp.where(row_id < ROWS // 2, a[1][j], a[2][j]) for j in range(3)]]
 
     greeted(0, 2)
     greet(1, 4)
     greeted(1, 4)
     greet(2, 8)
     arrive(k_copies)
-    stencil = wide(coefs, krow_r, kedge_r)
-
-    resid = each(lambda a, b: a - b, grad, hessian(warm))
+    coefs = dict(zip(NEIGHBOURS, wide(coefs, krow_r, kedge_r)))
+    resid = each(lambda a, b: a - b, grad, hessian(operator(source, half_obs, coefs), warm))
+    resid, diag = narrow(resid), narrow(diag)
+    op = operator([narrow(t) for t in source], narrow(half_obs), {n: narrow(t) for n, t in coefs.items()})
     dir0 = times(diag, resid)
-    img0 = hessian(dir0)
+    img0 = hessian(op, dir0)
     dir1 = times(diag, img0)
-    surf1 = to_surface(dir1)
+    surf1 = to_surface(op, dir1)
     smooth1 = smooth(dir1)
 
     def own_sum(fn):
@@ -471,13 +475,15 @@
         own_sum(lambda j: dir0[0][j] * img0[0][j]),
         own_sum(lambda j: img0[0][j] * dir1[0][j]),
         own_sum(
-            lambda j: obs[0][j] * (surf1[0][0][j] * surf1[0][0][j] + surf1[1][0][j] * surf1[1][0][j])
+            lambda j: half_obs[0][j] * (surf1[0][0][j] * surf1[0][0][j] + surf1[1][0][j] * surf1[1][0][j])
             + dir1[0][j] * smooth1[0][j]
         ),
     ]
     partial = jnp.zeros((ROWS, LANES), F32)
     for q, value in enumerate(dots):
         partial = jnp.where(row_id == q, value, partial)
+    partial = jnp.sum(partial, axis=1, keepdims=True)
+    partial = jnp.sum(jnp.where(lane_id // 32 == row_id, partial, 0.0), axis=0, keepdims=True)
 
     def exchange(value, stage_ref, recv_ref, send_sems, recv_sems, me, n, device):
         stage_ref[...] = value
@@ -497,7 +503,7 @@
     a_copies = exchange(
         partial, suma_s, suma_r, suma_send, suma_recv, mx, nx, lambda k: (lax.rem(mx + k, nx), my)
     )
-    img1 = plus(to_bed(surf1), smooth1)
+    img1 = plus(to_bed(op, surf1), smooth1)
     for copy in a_copies:
         copy.wait_recv()
     partial = suma_r[0]
@@ -512,8 +518,9 @@
     partial = sumb_r[0]
     for k in range(1, ny):
         partial = partial + sumb_r[k]
-    full = jnp.sum(partial, axis=1, keepdims=True)
-    s0, s1, s2, s3 = (jnp.broadcast_to(full[q : q + 1], (ROWS, LANES)) for q in range(4))
+    s0, s1, s2, s3 = (
+        jnp.broadcast_to(partial[:, 32 * q : 32 * q + 1], (ROWS, LANES)) for q in range(4)
+    )
 
     step0 = s0 / s1
     ratio = (step0 * step0 * s2 - s0) / s0
@@ -560,8 +567,8 @@
                 vmem(rows, LANES), vmem(6, rows, LANES),
                 vmem(8, rows, cols), vmem(2, 8, rows, cols),
                 vmem(rows, LANES), vmem(6, rows, LANES),
-                vmem(rows, LANES), vmem(nx, rows, LANES),
-                vmem(rows, LANES), vmem(ny, rows, LANES),
+                vmem(1, LANES), vmem(nx, 1, LANES),
+                vmem(1, LANES), vmem(ny, 1, LANES),
                 dma(8), dma(3, 2), dma(3, 2), dma(3, 6), dma(3, 6),
                 pltpu.SemaphoreType.REGULAR((3, 4)),
                 dma(nx), dma(nx), dma(ny), dma(ny),

time: 26.1 us -> 25.5 us (0.977)
  Pallas kernels: 24.8 us -> 24 us
    pallas_call x1, Pallas kernels: 24.8 us -> 24 us  [on_device(): call(grad, warm, eta, coef, slide, weight, ice, ground)]
where the time goes in v4:
time: 25.5 us; the launch traced here: 25.3 us
  Pallas kernels  24 us (94%)
  between operations  0.64 us (3%)
  other arithmetic  0.61 us (2%)
    pallas_call x1, Pallas kernels, on_device(): call(grad, warm, eta, coef, slide, weight, ice, ground)  24 us
    sub x1, other arithmetic, on_device(): return (sol + step * along, res - step * image)  0.61 us

profile of v4, /device:TPU:1, one launch (start us, length us, event | category | flops | bytes accessed | tf_op | source)
XLA Modules:
  0.0 25.3 jit_solution(13011146374128399474)
XLA Ops:
  0.6 24.0 %shard_map.95 = (f32[8,256]{1,0:T(8,128)S(1)}, f32[8,256]{1,0:T(8,128)S(1)}, f32[8,256]{1,0:T(8,128)S(1)}, f32[8,256]{1,0:T(8,128)S(1)}, f32[8,256]{1,0:T(8,128)S(1)}) custom-call(f32[8,256]{1,0:T(8,128)} %grad_h.1, f32[8,256]{1,0:T(8,128)} %warm_h.1, f32[32,8,256]{2,1,0:T(8,128)} %eta_h.1, f32[8,256]{1,0:T(8,128)} %coef_h.1, f32[2,8,256]{2,1,0:T(8,128)} %slide_h.1, ...), custom_call_target="tpu_custom_call" | custom-call | tf_op jit(solution)/shard_map/pallas_call | solution.py:578
  24.6 0.6 %multiply_subtract_fusion = (f32[8,256]{1,0:T(8,128)}, f32[8,256]{1,0:T(8,128)}) fusion(f32[8,256]{1,0:T(8,128)S(1)} %get-tuple-element.10, f32[8,256]{1,0:T(8,128)S(1)} %get-tuple-element.8, f32[8,256]{1,0:T(8,128)S(1)} %get-tuple-element.11, f32[8,256]{1,0:T(8,128)S(1)} %get-tuple-element.7, f32[8,256]{1,0:T(8,128)S(1)} %get-tuple-element.9), kind=kLoop, calls=%fused_computation | loop fusion | flops 8192 | bytes 57344 | tf_op jit(solution)/shard_map/sub | solution.py:579

commit v5 on v4

--- a/solution.py
+++ b/solution.py
@@ -43,11 +43,10 @@
     sol_o, res_o, step_o, along_o, image_o,
     grad_v, warm_v, eta_v, coef_v, slide_v, weight_v, ice_v, ground_v,
     w_v, wahead_v, wbehind_v, u_v, inva_v, pack_v,
-    wrow_s, wrow_r, wedge_s, wedge_r,
-    frow_s, frow_r, fedge_s, fedge_r,
+    first_s, first_r, edge_s, edge_r,
     krow_s, krow_r, kedge_s, kedge_r,
     suma_s, suma_r, sumb_s, sumb_r,
-    in_sem, row_send, row_recv, edge_send, edge_recv, known_sem, suma_send, suma_recv, sumb_send, sumb_recv,
+    local_sem, row_recv, edge_recv, known_sem, sum_send, suma_recv, sumb_recv,
     *, nx, ny, levels,
 ):
     mx = lax.axis_index("gx")
@@ -81,7 +80,7 @@
         (eta_h, eta_v), (coef_h, coef_v), (ground_h, ground_v), (ice_h, ice_v),
         (slide_h, slide_v), (weight_h, weight_v), (grad_h, grad_v), (warm_h, warm_v),
     ]
-    loads = [pltpu.make_async_copy(src, dst, in_sem.at[i]) for i, (src, dst) in enumerate(pairs)]
+    loads = [pltpu.make_async_copy(src, dst, local_sem.at[i]) for i, (src, dst) in enumerate(pairs)]
     for load in loads:
         load.start()
 
@@ -101,6 +100,7 @@
     friction = ground_v[...].astype(F32) * coef_v[...]
 
     slot = lambda z, f: 2 * (levels - 1 - z) + f
+    wtiles = 2 * levels // ROWS
 
     def pack_row(packed, value, row, m):
         parts = [row_roll(t, m % ROWS - row) for t in tiles(value)]
@@ -134,52 +134,17 @@
             last_rows = pack_row(last_rows, field, ROWS - 1, m)
             first_rows = pack_row(first_rows, field, 0, m)
             if m % ROWS == ROWS - 1:
-                put(wrow_s, (0, m // ROWS), last_rows)
-                put(wrow_s, (1, m // ROWS), first_rows)
+                put(first_s, (0, m // ROWS), last_rows)
+                put(first_s, (1, m // ROWS), first_rows)
             t0, t1 = tiles(field)
             ahead = lane_roll(t0, -1)
             behind = lane_roll(t1, 1)
             wahead_v[m] = ahead
             wbehind_v[m] = behind
             edge_packed = pack_lanes(edge_packed, jnp.where(low_half, behind, ahead), m)
-    wedge_s[...] = edge_packed
+    edge_s[0] = edge_packed
     total = flux + BED_DRAG * friction * w
     gain = 1.0 / total
-
-    def count(*offsets):
-        return 1 + sum(jnp.where(exists(*n), 1, 0) for n in offsets)
-
-    pl.semaphore_wait(barrier, count((1, 0), (-1, 0)) * count((0, 1), (0, -1)) - 1)
-
-    ends = []
-
-    def send(*copies):
-        for (dx, dy), copy in copies:
-            when(exists(dx, dy), copy.start)
-            ends.append((exists(dx, dy), copy))
-        return copies
-
-    def arrive(copies):
-        for (dx, dy), copy in copies:
-            when(exists(-dx, -dy), copy.wait_recv)
-
-    def exchange_edges(stage, edge, edge_in, row_of, rows_in):
-        out = []
-        for k, n in enumerate(SIDEWAYS):
-            out.append((n, pltpu.make_async_remote_copy(
-                src_ref=edge, dst_ref=edge_in.at[k],
-                send_sem=edge_send.at[stage, k], recv_sem=edge_recv.at[stage, k],
-                device_id=at(*n), device_id_type=MESH,
-            )))
-        for k, dx in enumerate((1, -1)):
-            out.append(((dx, 0), pltpu.make_async_remote_copy(
-                src_ref=row_of(k), dst_ref=rows_in.at[k],
-                send_sem=row_send.at[stage, k], recv_sem=row_recv.at[stage, k],
-                device_id=at(dx, 0), device_id_type=MESH,
-            )))
-        return send(*out)
-
-    w_copies = exchange_edges(0, wedge_s, wedge_r, lambda k: wrow_s.at[k], wrow_r)
 
     for load in loads[3:]:
         load.wait()
@@ -206,9 +171,60 @@
         return packed
 
     for f, value in enumerate(fields):
-        frow_s[f] = value
-    fedge_s[...] = pack_edges(fields)
-    f_copies = exchange_edges(1, fedge_s, fedge_r, lambda k: frow_s, frow_r)
+        for k in range(2):
+            put(first_s, (k, wtiles + f), tiles(value))
+    edge_s[1] = pack_edges(fields)
+
+    def count(*offsets):
+        return 1 + sum(jnp.where(exists(*n), 1, 0) for n in offsets)
+
+    pl.semaphore_wait(barrier, count((1, 0), (-1, 0)) * count((0, 1), (0, -1)) - 1)
+
+    def send(*copies):
+        for n, copy in copies:
+            when(exists(*n), copy.start)
+        return copies
+
+    def sent(copies):
+        for n, copy in copies:
+            when(exists(*n), copy.wait_send)
+
+    def arrive(copies):
+        for (dx, dy), copy in copies:
+            when(exists(-dx, -dy), copy.wait_recv)
+
+    def exchange_edges(stage, edge, edge_in, row_of, rows_in):
+        out = []
+        for k, n in enumerate(SIDEWAYS):
+            out.append((n, pltpu.make_async_remote_copy(
+                src_ref=edge, dst_ref=edge_in.at[k],
+                send_sem=local_sem.at[k], recv_sem=edge_recv.at[stage, k],
+                device_id=at(*n), device_id_type=MESH,
+            )))
+        for k, dx in enumerate((1, -1)):
+            out.append(((dx, 0), pltpu.make_async_remote_copy(
+                src_ref=row_of(k), dst_ref=rows_in.at[k],
+                send_sem=local_sem.at[6 + k], recv_sem=row_recv.at[stage, k],
+                device_id=at(dx, 0), device_id_type=MESH,
+            )))
+        return send(*out)
+
+    reaches = (1, 2, 4, 8)
+
+    def around(round):
+        reach = reaches[round]
+        return [n for n in ((reach, 0), (-reach, 0), (0, reach), (0, -reach)) if abs(n[0]) < nx and abs(n[1]) < ny]
+
+    def greet(round):
+        for n in around(round):
+            when(exists(*n), functools.partial(signal, known_sem.at[round], at(*n)))
+
+    def greeted(round):
+        pl.semaphore_wait(known_sem.at[round], count(*around(round)) - 1)
+
+    w_copies = exchange_edges(0, edge_s, edge_r, lambda k: first_s.at[k], first_r)
+    greet(0)
+
 
     u = jnp.ones((ROWS, 2 * LANES), F32)
     flux = SINK_RATE * eta_v[0] + BED_DRAG * friction
@@ -227,9 +243,9 @@
             keep = keep & flag
         return jnp.where(keep, value, 0.0)
 
-    def join_edges(ref, from_right):
+    def join_edges(ref, part, from_right):
         def got(dx, dy):
-            return ref[SIDEWAYS.index((-dx, -dy))]
+            return ref[SIDEWAYS.index((-dx, -dy)), part]
 
         own = jnp.where(
             from_right, inside(got(0, 1), has_right), inside(got(0, -1), has_left)
@@ -294,22 +310,15 @@
                         rolled = d_rolled if dy else s_rolled
                         add(sums, (dx, dy), j, rolled * by_lane[dy][j])
 
+    greeted(0)
+    greet(1)
+    sent(w_copies)
     arrive(w_copies)
-
-    def greet(round, reach):
-        for k, n in enumerate(((reach, 0), (-reach, 0), (0, reach), (0, -reach))):
-            if abs(n[0]) < nx and abs(n[1]) < ny:
-                when(exists(*n), functools.partial(signal, known_sem.at[round, k], at(*n)))
-
-    def greeted(round, reach):
-        for k, n in enumerate(((-reach, 0), (reach, 0), (0, -reach), (0, reach))):
-            if abs(n[0]) < nx and abs(n[1]) < ny:
-                when(exists(*n), functools.partial(pl.semaphore_wait, known_sem.at[round, k], 1))
-
-    greet(0, 2)
+    greeted(1)
+    greet(2)
 
     even_lane = lane_id % 2 == 0
-    e_own, e_up, e_down = join_edges(wedge_r, ~even_lane)
+    e_own, e_up, e_down = join_edges(edge_r, 0, ~even_lane)
     e_beyond = jnp.where(row_id < 4, e_up, e_down)
     edge_of = {
         0: e_own,
@@ -327,7 +336,7 @@
     for side, flag in ((0, has_down), (1, has_up)):
         dx = 2 * side - 1
         for g in range(2 * levels // ROWS):
-            t0, t1 = tiles(inside(wrow_r[side, g], flag))
+            t0, t1 = tiles(inside(first_r[side, g], flag))
             plus_pair, minus_pair = seam(
                 lane_roll(t0, -1), lane_roll(t1, -1), lane_roll(t0, 1), lane_roll(t1, 1)
             )
@@ -353,27 +362,26 @@
         coefs.append(jnp.concatenate(pair, axis=1))
         krow_s[i, :, :LANES] = pair[0]
         krow_s[i, :, LANES:] = pair[1]
-    kedge_s[...] = pack_edges(coefs)
-    k_copies = exchange_edges(2, kedge_s, kedge_r, lambda k: krow_s, krow_r)
+    kedge_s[0] = pack_edges(coefs)
+    k_copies = exchange_edges(1, kedge_s, kedge_r, lambda k: krow_s, krow_r)
 
     group_right = lane_id % 16 < 8
 
-    def wide(values, row_ref, edge_ref):
-        joined = join_edges(edge_ref, group_right)
+    def wide(values, row_ref, start, edge_ref, part):
+        joined = join_edges(edge_ref, part, group_right)
         out = []
         for f, value in enumerate(values):
             rows = [
                 tiles(value),
-                tiles(inside(row_ref[1, f], has_up)),
-                tiles(inside(row_ref[0, f], has_down)),
+                tiles(inside(row_ref[1, start + f], has_up)),
+                tiles(inside(row_ref[0, start + f], has_down)),
             ]
             out.append(
                 [rows[i] + [lane_roll(joined[i], -16 * f)] for i in range(3)]
             )
         return out
 
-    arrive(f_copies)
-    *source, half_obs, diag, grad, warm = wide(fields, frow_r, fedge_r)
+    *source, half_obs, diag, grad, warm = wide(fields, first_r, wtiles, edge_r, 1)
 
     def each(fn, *args):
         return [[fn(*(a[i][j] for a in args)) for j in range(3)] for i in range(len(args[0]))]
@@ -451,12 +459,10 @@
     def narrow(a):
         return [a[0], [jnp.where(row_id < ROWS // 2, a[1][j], a[2][j]) for j in range(3)]]
 
-    greeted(0, 2)
-    greet(1, 4)
-    greeted(1, 4)
-    greet(2, 8)
+    greeted(2)
+    greet(3)
     arrive(k_copies)
-    coefs = dict(zip(NEIGHBOURS, wide(coefs, krow_r, kedge_r)))
+    coefs = dict(zip(NEIGHBOURS, wide(coefs, krow_r, 0, kedge_r, 0)))
     resid = each(lambda a, b: a - b, grad, hessian(operator(source, half_obs, coefs), warm))
     resid, diag = narrow(resid), narrow(diag)
     op = operator([narrow(t) for t in source], narrow(half_obs), {n: narrow(t) for n, t in coefs.items()})
@@ -485,39 +491,34 @@
     partial = jnp.sum(partial, axis=1, keepdims=True)
     partial = jnp.sum(jnp.where(lane_id // 32 == row_id, partial, 0.0), axis=0, keepdims=True)
 
-    def exchange(value, stage_ref, recv_ref, send_sems, recv_sems, me, n, device):
+    def spread_sums(value, stage_ref, recv_ref, send_sem, recv_sem, me, n, device):
         stage_ref[...] = value
-        out = []
         for k in range(1, n):
-            copy = pltpu.make_async_remote_copy(
-                src_ref=stage_ref, dst_ref=recv_ref.at[me],
-                send_sem=send_sems.at[k], recv_sem=recv_sems.at[k],
+            pltpu.make_async_remote_copy(
+                src_ref=stage_ref, dst_ref=recv_ref.at[me], send_sem=send_sem, recv_sem=recv_sem,
                 device_id=device(k), device_id_type=MESH,
-            )
-            copy.start()
-            out.append(copy)
-            ends.append((None, copy))
+            ).start()
         recv_ref[me] = value
-        return out
-
-    a_copies = exchange(
-        partial, suma_s, suma_r, suma_send, suma_recv, mx, nx, lambda k: (lax.rem(mx + k, nx), my)
-    )
+
+    def all_sent(sem, ref, n):
+        whole = ref.at[pl.ds(0, n - 1)]
+        pltpu.make_async_copy(whole, whole, sem).wait()
+
+    def gather_sums(ref, sem, n):
+        all_sent(sem, ref, n)
+        value = ref[0]
+        for k in range(1, n):
+            value = value + ref[k]
+        return value
+
+    spread_sums(partial, suma_s, suma_r, sum_send, suma_recv, mx, nx, lambda k: (lax.rem(mx + k, nx), my))
     img1 = plus(to_bed(op, surf1), smooth1)
-    for copy in a_copies:
-        copy.wait_recv()
-    partial = suma_r[0]
-    for k in range(1, nx):
-        partial = partial + suma_r[k]
-    greeted(2, 8)
-    b_copies = exchange(
-        partial, sumb_s, sumb_r, sumb_send, sumb_recv, my, ny, lambda k: (mx, lax.rem(my + k, ny))
-    )
-    for copy in b_copies:
-        copy.wait_recv()
-    partial = sumb_r[0]
-    for k in range(1, ny):
-        partial = partial + sumb_r[k]
+    sent(k_copies)
+    partial = gather_sums(suma_r, suma_recv, nx)
+    greeted(3)
+    all_sent(sum_send, suma_r, nx)
+    spread_sums(partial, sumb_s, sumb_r, sum_send, sumb_recv, my, ny, lambda k: (mx, lax.rem(my + k, ny)))
+    partial = gather_sums(sumb_r, sumb_recv, ny)
     s0, s1, s2, s3 = (
         jnp.broadcast_to(partial[:, 32 * q : 32 * q + 1], (ROWS, LANES)) for q in range(4)
     )
@@ -535,11 +536,7 @@
         along_o[:, cols] = grow * dir0[0][j] - step0 * dir1[0][j]
         image_o[:, cols] = grow * img0[0][j] - step0 * img1[0][j]
 
-    for flag, copy in ends:
-        if flag is None:
-            copy.wait_send()
-        else:
-            when(flag, copy.wait_send)
+    all_sent(sum_send, sumb_r, ny)
 
 
 def solution(mesh):
@@ -561,17 +558,13 @@
                 pltpu.VMEM((rows, cols), jnp.int32), pltpu.VMEM((rows, cols), jnp.int32),
                 vmem(2 * levels, rows, cols), vmem(2 * levels, rows, LANES), vmem(2 * levels, rows, LANES),
                 vmem(levels, rows, cols), vmem(levels, rows, cols), vmem(2, 2, wtiles, rows, cols),
-                vmem(2, wtiles, rows, cols), vmem(2, wtiles, rows, cols),
-                vmem(rows, LANES), vmem(6, rows, LANES),
-                vmem(6, rows, cols), vmem(2, 6, rows, cols),
-                vmem(rows, LANES), vmem(6, rows, LANES),
+                vmem(2, wtiles + 6, rows, cols), vmem(2, wtiles + 6, rows, cols),
+                vmem(2, rows, LANES), vmem(6, 2, rows, LANES),
                 vmem(8, rows, cols), vmem(2, 8, rows, cols),
-                vmem(rows, LANES), vmem(6, rows, LANES),
+                vmem(1, rows, LANES), vmem(6, 1, rows, LANES),
                 vmem(1, LANES), vmem(nx, 1, LANES),
                 vmem(1, LANES), vmem(ny, 1, LANES),
-                dma(8), dma(3, 2), dma(3, 2), dma(3, 6), dma(3, 6),
-                pltpu.SemaphoreType.REGULAR((3, 4)),
-                dma(nx), dma(nx), dma(ny), dma(ny),
+                dma(8), dma(2, 2), dma(2, 6), pltpu.SemaphoreType.REGULAR((4,)), dma(), dma(), dma(),
             ],
             compiler_params=pltpu.CompilerParams(collective_id=0, has_side_effects=True),
         )

time: 25.5 us -> 25 us (0.980)
  Pallas kernels: 24 us -> 23.4 us
    pallas_call x1, Pallas kernels: 24 us -> 23.4 us  [on_device(): call(grad, warm, eta, coef, slide, weight, ice, ground)]
where the time goes in v5:
time: 25 us; the launch traced here: 24.7 us
  Pallas kernels  23.4 us (94%)
  between operations  0.64 us (3%)
  other arithmetic  0.61 us (2%)
    pallas_call x1, Pallas kernels, on_device(): call(grad, warm, eta, coef, slide, weight, ice, ground)  23.4 us
    sub x1, other arithmetic, on_device(): return (sol + step * along, res - step * image)  0.61 us

profile of v5, /device:TPU:1, one launch (start us, length us, event | category | flops | bytes accessed | tf_op | source)
XLA Modules:
  0.0 24.7 jit_solution(649541079971889740)
XLA Ops:
  0.6 23.4 %shard_map.95 = (f32[8,256]{1,0:T(8,128)S(1)}, f32[8,256]{1,0:T(8,128)S(1)}, f32[8,256]{1,0:T(8,128)S(1)}, f32[8,256]{1,0:T(8,128)S(1)}, f32[8,256]{1,0:T(8,128)S(1)}) custom-call(f32[8,256]{1,0:T(8,128)} %grad_h.1, f32[8,256]{1,0:T(8,128)} %warm_h.1, f32[32,8,256]{2,1,0:T(8,128)} %eta_h.1, f32[8,256]{1,0:T(8,128)} %coef_h.1, f32[2,8,256]{2,1,0:T(8,128)} %slide_h.1, ...), custom_call_target="tpu_custom_call" | custom-call | tf_op jit(solution)/shard_map/pallas_call | solution.py:571
  24.1 0.6 %multiply_subtract_fusion = (f32[8,256]{1,0:T(8,128)}, f32[8,256]{1,0:T(8,128)}) fusion(f32[8,256]{1,0:T(8,128)S(1)} %get-tuple-element.10, f32[8,256]{1,0:T(8,128)S(1)} %get-tuple-element.8, f32[8,256]{1,0:T(8,128)S(1)} %get-tuple-element.11, f32[8,256]{1,0:T(8,128)S(1)} %get-tuple-element.7, f32[8,256]{1,0:T(8,128)S(1)} %get-tuple-element.9), kind=kLoop, calls=%fused_computation | loop fusion | flops 8192 | bytes 57344 | tf_op jit(solution)/shard_map/sub | solution.py:572

commit v6 on v5

--- a/solution.py
+++ b/solution.py
@@ -45,8 +45,8 @@
     w_v, wahead_v, wbehind_v, u_v, inva_v, pack_v,
     first_s, first_r, edge_s, edge_r,
     krow_s, krow_r, kedge_s, kedge_r,
-    suma_s, suma_r, sumb_s, sumb_r,
-    local_sem, row_recv, edge_recv, known_sem, sum_send, suma_recv, sumb_recv,
+    sum_s, sum_r,
+    local_sem, row_recv, edge_recv, known_sem, sum_send, sum_recv,
     *, nx, ny, levels,
 ):
     mx = lax.axis_index("gx")
@@ -213,7 +213,7 @@
 
     def around(round):
         reach = reaches[round]
-        return [n for n in ((reach, 0), (-reach, 0), (0, reach), (0, -reach)) if abs(n[0]) < nx and abs(n[1]) < ny]
+        return [(dx * reach, dy * reach) for dx, dy in NEIGHBOURS if abs(dx) * reach < nx and abs(dy) * reach < ny]
 
     def greet(round):
         for n in around(round):
@@ -314,8 +314,6 @@
     greet(1)
     sent(w_copies)
     arrive(w_copies)
-    greeted(1)
-    greet(2)
 
     even_lane = lane_id % 2 == 0
     e_own, e_up, e_down = join_edges(edge_r, 0, ~even_lane)
@@ -365,6 +363,9 @@
     kedge_s[0] = pack_edges(coefs)
     k_copies = exchange_edges(1, kedge_s, kedge_r, lambda k: krow_s, krow_r)
 
+    greeted(1)
+    greet(2)
+
     group_right = lane_id % 16 < 8
 
     def wide(values, row_ref, start, edge_ref, part):
@@ -491,15 +492,6 @@
     partial = jnp.sum(partial, axis=1, keepdims=True)
     partial = jnp.sum(jnp.where(lane_id // 32 == row_id, partial, 0.0), axis=0, keepdims=True)
 
-    def spread_sums(value, stage_ref, recv_ref, send_sem, recv_sem, me, n, device):
-        stage_ref[...] = value
-        for k in range(1, n):
-            pltpu.make_async_remote_copy(
-                src_ref=stage_ref, dst_ref=recv_ref.at[me], send_sem=send_sem, recv_sem=recv_sem,
-                device_id=device(k), device_id_type=MESH,
-            ).start()
-        recv_ref[me] = value
-
     def all_sent(sem, ref, n):
         whole = ref.at[pl.ds(0, n - 1)]
         pltpu.make_async_copy(whole, whole, sem).wait()
@@ -511,14 +503,23 @@
             value = value + ref[k]
         return value
 
-    spread_sums(partial, suma_s, suma_r, sum_send, suma_recv, mx, nx, lambda k: (lax.rem(mx + k, nx), my))
+    sum_s[...] = partial
+    me = my * nx + mx
+    greeted(3)
+    circ = lambda v, n: min(v % n, n - v % n)
+    far = lambda o: circ(o[0] / 2, nx // 2) + circ(o[1] % 4, 4) + circ(o[1] // 4, 4)
+    offsets = sorted(
+        [(i, j) for i in range(nx) for j in range(ny) if (i, j) != (0, 0)], key=far, reverse=True
+    )
+    for i, j in offsets:
+        pltpu.make_async_remote_copy(
+            src_ref=sum_s, dst_ref=sum_r.at[me], send_sem=sum_send, recv_sem=sum_recv,
+            device_id=(lax.rem(mx + i, nx), lax.rem(my + j, ny)), device_id_type=MESH,
+        ).start()
+    sum_r[me] = partial
     img1 = plus(to_bed(op, surf1), smooth1)
     sent(k_copies)
-    partial = gather_sums(suma_r, suma_recv, nx)
-    greeted(3)
-    all_sent(sum_send, suma_r, nx)
-    spread_sums(partial, sumb_s, sumb_r, sum_send, sumb_recv, my, ny, lambda k: (mx, lax.rem(my + k, ny)))
-    partial = gather_sums(sumb_r, sumb_recv, ny)
+    partial = gather_sums(sum_r, sum_recv, nx * ny)
     s0, s1, s2, s3 = (
         jnp.broadcast_to(partial[:, 32 * q : 32 * q + 1], (ROWS, LANES)) for q in range(4)
     )
@@ -536,7 +537,7 @@
         along_o[:, cols] = grow * dir0[0][j] - step0 * dir1[0][j]
         image_o[:, cols] = grow * img0[0][j] - step0 * img1[0][j]
 
-    all_sent(sum_send, sumb_r, ny)
+    all_sent(sum_send, sum_r, nx * ny)
 
 
 def solution(mesh):
@@ -562,9 +563,8 @@
                 vmem(2, rows, LANES), vmem(6, 2, rows, LANES),
                 vmem(8, rows, cols), vmem(2, 8, rows, cols),
                 vmem(1, rows, LANES), vmem(6, 1, rows, LANES),
-                vmem(1, LANES), vmem(nx, 1, LANES),
-                vmem(1, LANES), vmem(ny, 1, LANES),
-                dma(8), dma(2, 2), dma(2, 6), pltpu.SemaphoreType.REGULAR((4,)), dma(), dma(), dma(),
+                vmem(1, LANES), vmem(nx * ny, 1, LANES),
+                dma(8), dma(2, 2), dma(2, 6), pltpu.SemaphoreType.REGULAR((4,)), dma(), dma(),
             ],
             compiler_params=pltpu.CompilerParams(collective_id=0, has_side_effects=True),
         )

time: 25 us -> 24 us (0.960); the launches traced: 24.7 us -> 23.9 us
  Pallas kernels: 23.4 us -> 22.7 us
    pallas_call x1, Pallas kernels: 23.4 us -> 22.7 us  [on_device(): call(grad, warm, eta, coef, slide, weight, ice, ground)]
where the time goes in v6:
time: 24 us; the launch traced here: 23.9 us
  Pallas kernels  22.7 us (95%)
  between operations  0.64 us (3%)
  other arithmetic  0.61 us (3%)
    pallas_call x1, Pallas kernels, on_device(): call(grad, warm, eta, coef, slide, weight, ice, ground)  22.7 us
    sub x1, other arithmetic, on_device(): return (sol + step * along, res - step * image)  0.61 us

profile of v6, /device:TPU:1, one launch (start us, length us, event | category | flops | bytes accessed | tf_op | source)
XLA Modules:
  0.0 23.9 jit_solution(14594677983336085544)
XLA Ops:
  0.6 22.7 %shard_map.95 = (f32[8,256]{1,0:T(8,128)S(1)}, f32[8,256]{1,0:T(8,128)S(1)}, f32[8,256]{1,0:T(8,128)S(1)}, f32[8,256]{1,0:T(8,128)S(1)}, f32[8,256]{1,0:T(8,128)S(1)}) custom-call(f32[8,256]{1,0:T(8,128)} %grad_h.1, f32[8,256]{1,0:T(8,128)} %warm_h.1, f32[32,8,256]{2,1,0:T(8,128)} %eta_h.1, f32[8,256]{1,0:T(8,128)} %coef_h.1, f32[2,8,256]{2,1,0:T(8,128)} %slide_h.1, ...), custom_call_target="tpu_custom_call" | custom-call | tf_op jit(solution)/shard_map/pallas_call | solution.py:571
  23.3 0.6 %multiply_subtract_fusion = (f32[8,256]{1,0:T(8,128)}, f32[8,256]{1,0:T(8,128)}) fusion(f32[8,256]{1,0:T(8,128)S(1)} %get-tuple-element.10, f32[8,256]{1,0:T(8,128)S(1)} %get-tuple-element.8, f32[8,256]{1,0:T(8,128)S(1)} %get-tuple-element.11, f32[8,256]{1,0:T(8,128)S(1)} %get-tuple-element.7, f32[8,256]{1,0:T(8,128)S(1)} %get-tuple-element.9), kind=kLoop, calls=%fused_computation | loop fusion | flops 8192 | bytes 57344 | tf_op jit(solution)/shard_map/sub | solution.py:572

commit v7 on v6

--- a/solution.py
+++ b/solution.py
@@ -46,7 +46,7 @@
     first_s, first_r, edge_s, edge_r,
     krow_s, krow_r, kedge_s, kedge_r,
     sum_s, sum_r,
-    local_sem, row_recv, edge_recv, known_sem, sum_send, sum_recv,
+    load_sem, send_sem, recv_sem, known_sem, sum_send, sum_recv,
     *, nx, ny, levels,
 ):
     mx = lax.axis_index("gx")
@@ -80,9 +80,12 @@
         (eta_h, eta_v), (coef_h, coef_v), (ground_h, ground_v), (ice_h, ice_v),
         (slide_h, slide_v), (weight_h, weight_v), (grad_h, grad_v), (warm_h, warm_v),
     ]
-    loads = [pltpu.make_async_copy(src, dst, local_sem.at[i]) for i, (src, dst) in enumerate(pairs)]
-    for load in loads:
-        load.start()
+    for i, (src, dst) in enumerate(pairs):
+        pltpu.make_async_copy(src, dst, load_sem.at[0 if i < 3 else 1]).start()
+
+    def settle(ref, count, sem):
+        whole = ref.at[pl.ds(0, count)]
+        pltpu.make_async_copy(whole, whole, sem).wait()
 
     row_id = lax.broadcasted_iota(jnp.int32, (ROWS, LANES), 0)
     lane_id = lax.broadcasted_iota(jnp.int32, (ROWS, LANES), 1)
@@ -95,8 +98,7 @@
     def tiles(value):
         return [value[:, :LANES], value[:, LANES:]]
 
-    for load in loads[:3]:
-        load.wait()
+    settle(w_v, levels + 2, load_sem.at[0])
     friction = ground_v[...].astype(F32) * coef_v[...]
 
     slot = lambda z, f: 2 * (levels - 1 - z) + f
@@ -146,8 +148,7 @@
     total = flux + BED_DRAG * friction * w
     gain = 1.0 / total
 
-    for load in loads[3:]:
-        load.wait()
+    settle(w_v, 6, load_sem.at[1])
     ice = ice_v[...].astype(F32)
     coef = coef_v[...]
     stuck = ice * ground_v[...].astype(F32)
@@ -180,34 +181,27 @@
 
     pl.semaphore_wait(barrier, count((1, 0), (-1, 0)) * count((0, 1), (0, -1)) - 1)
 
-    def send(*copies):
-        for n, copy in copies:
-            when(exists(*n), copy.start)
-        return copies
-
-    def sent(copies):
-        for n, copy in copies:
-            when(exists(*n), copy.wait_send)
-
-    def arrive(copies):
-        for (dx, dy), copy in copies:
-            when(exists(-dx, -dy), copy.wait_recv)
+    def all_neighbours(ref, per_row, per_edge, sem):
+        for beside in (1, 2):
+            for aside in (1, 2):
+                many_rows = exists(1, 0) & exists(-1, 0) if beside == 2 else ~(exists(1, 0) & exists(-1, 0))
+                many_edges = exists(0, 1) & exists(0, -1) if aside == 2 else ~(exists(0, 1) & exists(0, -1))
+                size = beside * per_row + (beside + 1) * aside * per_edge
+                when(many_rows & many_edges, functools.partial(settle, ref, size, sem))
 
     def exchange_edges(stage, edge, edge_in, row_of, rows_in):
-        out = []
         for k, n in enumerate(SIDEWAYS):
-            out.append((n, pltpu.make_async_remote_copy(
+            when(exists(*n), pltpu.make_async_remote_copy(
                 src_ref=edge, dst_ref=edge_in.at[k],
-                send_sem=local_sem.at[k], recv_sem=edge_recv.at[stage, k],
+                send_sem=send_sem.at[stage], recv_sem=recv_sem.at[stage],
                 device_id=at(*n), device_id_type=MESH,
-            )))
+            ).start)
         for k, dx in enumerate((1, -1)):
-            out.append(((dx, 0), pltpu.make_async_remote_copy(
+            when(exists(dx, 0), pltpu.make_async_remote_copy(
                 src_ref=row_of(k), dst_ref=rows_in.at[k],
-                send_sem=local_sem.at[6 + k], recv_sem=row_recv.at[stage, k],
+                send_sem=send_sem.at[stage], recv_sem=recv_sem.at[stage],
                 device_id=at(dx, 0), device_id_type=MESH,
-            )))
-        return send(*out)
+            ).start)
 
     reaches = (1, 2, 4, 8)
 
@@ -222,7 +216,7 @@
     def greeted(round):
         pl.semaphore_wait(known_sem.at[round], count(*around(round)) - 1)
 
-    w_copies = exchange_edges(0, edge_s, edge_r, lambda k: first_s.at[k], first_r)
+    exchange_edges(0, edge_s, edge_r, lambda k: first_s.at[k], first_r)
     greet(0)
 
 
@@ -312,8 +306,8 @@
 
     greeted(0)
     greet(1)
-    sent(w_copies)
-    arrive(w_copies)
+    all_neighbours(w_v, wtiles + 6, 1, send_sem.at[0])
+    all_neighbours(w_v, wtiles + 6, 1, recv_sem.at[0])
 
     even_lane = lane_id % 2 == 0
     e_own, e_up, e_down = join_edges(edge_r, 0, ~even_lane)
@@ -361,7 +355,7 @@
         krow_s[i, :, :LANES] = pair[0]
         krow_s[i, :, LANES:] = pair[1]
     kedge_s[0] = pack_edges(coefs)
-    k_copies = exchange_edges(1, kedge_s, kedge_r, lambda k: krow_s, krow_r)
+    exchange_edges(1, kedge_s, kedge_r, lambda k: krow_s, krow_r)
 
     greeted(1)
     greet(2)
@@ -462,7 +456,7 @@
 
     greeted(2)
     greet(3)
-    arrive(k_copies)
+    all_neighbours(wahead_v, 16, 1, recv_sem.at[1])
     coefs = dict(zip(NEIGHBOURS, wide(coefs, krow_r, 0, kedge_r, 0)))
     resid = each(lambda a, b: a - b, grad, hessian(operator(source, half_obs, coefs), warm))
     resid, diag = narrow(resid), narrow(diag)
@@ -492,12 +486,8 @@
     partial = jnp.sum(partial, axis=1, keepdims=True)
     partial = jnp.sum(jnp.where(lane_id // 32 == row_id, partial, 0.0), axis=0, keepdims=True)
 
-    def all_sent(sem, ref, n):
-        whole = ref.at[pl.ds(0, n - 1)]
-        pltpu.make_async_copy(whole, whole, sem).wait()
-
     def gather_sums(ref, sem, n):
-        all_sent(sem, ref, n)
+        settle(ref, n - 1, sem)
         value = ref[0]
         for k in range(1, n):
             value = value + ref[k]
@@ -518,7 +508,7 @@
         ).start()
     sum_r[me] = partial
     img1 = plus(to_bed(op, surf1), smooth1)
-    sent(k_copies)
+    all_neighbours(wahead_v, 16, 1, send_sem.at[1])
     partial = gather_sums(sum_r, sum_recv, nx * ny)
     s0, s1, s2, s3 = (
         jnp.broadcast_to(partial[:, 32 * q : 32 * q + 1], (ROWS, LANES)) for q in range(4)
@@ -537,7 +527,7 @@
         along_o[:, cols] = grow * dir0[0][j] - step0 * dir1[0][j]
         image_o[:, cols] = grow * img0[0][j] - step0 * img1[0][j]
 
-    all_sent(sum_send, sum_r, nx * ny)
+    settle(sum_r, nx * ny - 1, sum_send)
 
 
 def solution(mesh):
@@ -564,7 +554,7 @@
                 vmem(8, rows, cols), vmem(2, 8, rows, cols),
                 vmem(1, rows, LANES), vmem(6, 1, rows, LANES),
                 vmem(1, LANES), vmem(nx * ny, 1, LANES),
-                dma(8), dma(2, 2), dma(2, 6), pltpu.SemaphoreType.REGULAR((4,)), dma(), dma(),
+                dma(2), dma(2), dma(2), pltpu.SemaphoreType.REGULAR((4,)), dma(), dma(),
             ],
             compiler_params=pltpu.CompilerParams(collective_id=0, has_side_effects=True),
         )

time: 24 us -> 23.9 us (level)
  no operation moved by 1% of the time
where the time goes in v7:
time: 23.9 us; the launch traced here: 23.8 us
  Pallas kernels  22.5 us (94%)
  between operations  0.64 us (3%)
  other arithmetic  0.61 us (3%)
    pallas_call x1, Pallas kernels, on_device(): call(grad, warm, eta, coef, slide, weight, ice, ground)  22.5 us
    sub x1, other arithmetic, on_device(): return (sol + step * along, res - step * image)  0.61 us

profile of v7, /device:TPU:1, one launch (start us, length us, event | category | flops | bytes accessed | tf_op | source)
XLA Modules:
  0.0 23.8 jit_solution(2758915140884743403)
XLA Ops:
  0.6 22.5 %shard_map.95 = (f32[8,256]{1,0:T(8,128)S(1)}, f32[8,256]{1,0:T(8,128)S(1)}, f32[8,256]{1,0:T(8,128)S(1)}, f32[8,256]{1,0:T(8,128)S(1)}, f32[8,256]{1,0:T(8,128)S(1)}) custom-call(f32[8,256]{1,0:T(8,128)} %grad_h.1, f32[8,256]{1,0:T(8,128)} %warm_h.1, f32[32,8,256]{2,1,0:T(8,128)} %eta_h.1, f32[8,256]{1,0:T(8,128)} %coef_h.1, f32[2,8,256]{2,1,0:T(8,128)} %slide_h.1, ...), custom_call_target="tpu_custom_call" | custom-call | tf_op jit(solution)/shard_map/pallas_call | solution.py:561
  23.2 0.6 %multiply_subtract_fusion = (f32[8,256]{1,0:T(8,128)}, f32[8,256]{1,0:T(8,128)}) fusion(f32[8,256]{1,0:T(8,128)S(1)} %get-tuple-element.10, f32[8,256]{1,0:T(8,128)S(1)} %get-tuple-element.8, f32[8,256]{1,0:T(8,128)S(1)} %get-tuple-element.11, f32[8,256]{1,0:T(8,128)S(1)} %get-tuple-element.7, f32[8,256]{1,0:T(8,128)S(1)} %get-tuple-element.9), kind=kLoop, calls=%fused_computation | loop fusion | flops 8192 | bytes 57344 | tf_op jit(solution)/shard_map/sub | solution.py:562

commit v8 on v7

--- a/solution.py
+++ b/solution.py
@@ -488,10 +488,12 @@
 
     def gather_sums(ref, sem, n):
         settle(ref, n - 1, sem)
-        value = ref[0]
-        for k in range(1, n):
-            value = value + ref[k]
-        return value
+        parts = [ref[k] for k in range(min(8, n))]
+        for k in range(8, n):
+            parts[k % 8] = parts[k % 8] + ref[k]
+        while len(parts) > 1:
+            parts = [functools.reduce(lambda a, b: a + b, parts[k : k + 2]) for k in range(0, len(parts), 2)]
+        return parts[0]
 
     sum_s[...] = partial
     me = my * nx + mx

time: 23.9 us -> 23.8 us (level)
  no operation moved by 1% of the time
where the time goes in v8:
time: 23.8 us; the launch traced here: 23.7 us
  Pallas kernels  22.4 us (94%)
  between operations  0.64 us (3%)
  other arithmetic  0.61 us (3%)
    pallas_call x1, Pallas kernels, on_device(): call(grad, warm, eta, coef, slide, weight, ice, ground)  22.4 us
    sub x1, other arithmetic, on_device(): return (sol + step * along, res - step * image)  0.61 us

profile of v8, /device:TPU:1, one launch (start us, length us, event | category | flops | bytes accessed | tf_op | source)
XLA Modules:
  0.0 23.7 jit_solution(3651002162234436184)
XLA Ops:
  0.6 22.4 %shard_map.95 = (f32[8,256]{1,0:T(8,128)S(1)}, f32[8,256]{1,0:T(8,128)S(1)}, f32[8,256]{1,0:T(8,128)S(1)}, f32[8,256]{1,0:T(8,128)S(1)}, f32[8,256]{1,0:T(8,128)S(1)}) custom-call(f32[8,256]{1,0:T(8,128)} %grad_h.1, f32[8,256]{1,0:T(8,128)} %warm_h.1, f32[32,8,256]{2,1,0:T(8,128)} %eta_h.1, f32[8,256]{1,0:T(8,128)} %coef_h.1, f32[2,8,256]{2,1,0:T(8,128)} %slide_h.1, ...), custom_call_target="tpu_custom_call" | custom-call | tf_op jit(solution)/shard_map/pallas_call | solution.py:563
  23.0 0.6 %multiply_subtract_fusion = (f32[8,256]{1,0:T(8,128)}, f32[8,256]{1,0:T(8,128)}) fusion(f32[8,256]{1,0:T(8,128)S(1)} %get-tuple-element.10, f32[8,256]{1,0:T(8,128)S(1)} %get-tuple-element.8, f32[8,256]{1,0:T(8,128)S(1)} %get-tuple-element.11, f32[8,256]{1,0:T(8,128)S(1)} %get-tuple-element.7, f32[8,256]{1,0:T(8,128)S(1)} %get-tuple-element.9), kind=kLoop, calls=%fused_computation | loop fusion | flops 8192 | bytes 57344 | tf_op jit(solution)/shard_map/sub | solution.py:564

commit v9 on v8

--- a/solution.py
+++ b/solution.py
@@ -405,10 +405,29 @@
     def times(a, b):
         return each(lambda s, t: s * t, a, b)
 
+    def narrow(a):
+        return [a[0], [jnp.where(row_id < ROWS // 2, a[1][j], a[2][j]) for j in range(3)]]
+
+    def from_row_narrow(a, dx):
+        if len(a) == 2:
+            return from_row(a, dx)
+        if dx == 0:
+            return narrow(a)
+        mask, last_up = (row_first, ROWS // 2) if dx > 0 else (row_last, ROWS // 2 - 2)
+        beyond = [jnp.where(row_id <= last_up, a[1][j], a[2][j]) for j in range(3)]
+        return [
+            [row_roll(jnp.where(mask, a[dx % 3][j], a[0][j]), -dx) for j in range(3)],
+            [row_roll(jnp.where(mask, a[0][j], beyond[j]), -dx) for j in range(3)],
+        ]
+
+    def inner(a):
+        return from_row_narrow(a, 0)
+
     def smooth(q):
         return each(
             lambda c, a, b, d, e: REG_GAMMA * (c + REG_SMOOTH * (4.0 * c - (a + b + d + e))),
-            q, from_row(q, 1), from_row(q, -1), from_lane(q, 1), from_lane(q, -1),
+            inner(q), from_row_narrow(q, 1), from_row_narrow(q, -1),
+            from_lane(inner(q), 1), from_lane(inner(q), -1),
         )
 
     def to_surface(op, q):
@@ -428,15 +447,15 @@
         out = []
         for c in range(2):
             traction = times(op.half_obs, surface[c])
-            result = traction
+            result = inner(traction)
             for dy in (-1, 0, 1):
                 gathered = None
                 for dx in (-1, 0, 1):
                     if (dx, dy) != (0, 0):
-                        term = from_row(times(op.stencil[c][-dx, -dy], traction), dx)
+                        term = from_row_narrow(times(op.stencil[c][-dx, -dy], traction), dx)
                         gathered = term if gathered is None else plus(gathered, term)
                 result = plus(result, from_lane(gathered, dy))
-            out.append(times(op.source[c], result))
+            out.append(times(inner(op.source[c]), result))
         return plus(*out)
 
     def hessian(op, q):
@@ -451,15 +470,12 @@
             for sign in (1, -1)
         ])
 
-    def narrow(a):
-        return [a[0], [jnp.where(row_id < ROWS // 2, a[1][j], a[2][j]) for j in range(3)]]
-
     greeted(2)
     greet(3)
     all_neighbours(wahead_v, 16, 1, recv_sem.at[1])
     coefs = dict(zip(NEIGHBOURS, wide(coefs, krow_r, 0, kedge_r, 0)))
-    resid = each(lambda a, b: a - b, grad, hessian(operator(source, half_obs, coefs), warm))
-    resid, diag = narrow(resid), narrow(diag)
+    resid = each(lambda a, b: a - b, narrow(grad), hessian(operator(source, half_obs, coefs), warm))
+    diag = narrow(diag)
     op = operator([narrow(t) for t in source], narrow(half_obs), {n: narrow(t) for n, t in coefs.items()})
     dir0 = times(diag, resid)
     img0 = hessian(op, dir0)

time: 23.8 us -> 23.8 us (level)
  no operation moved by 1% of the time
where the time goes in v9:
time: 23.8 us; the launch traced here: 23.7 us
  Pallas kernels  22.4 us (94%)
  between operations  0.64 us (3%)
  other arithmetic  0.61 us (3%)
    pallas_call x1, Pallas kernels, on_device(): call(grad, warm, eta, coef, slide, weight, ice, ground)  22.4 us
    sub x1, other arithmetic, on_device(): return (sol + step * along, res - step * image)  0.61 us

profile of v9, /device:TPU:1, one launch (start us, length us, event | category | flops | bytes accessed | tf_op | source)
XLA Modules:
  0.0 23.7 jit_solution(6255346154234307028)
XLA Ops:
  0.6 22.4 %shard_map.95 = (f32[8,256]{1,0:T(8,128)S(1)}, f32[8,256]{1,0:T(8,128)S(1)}, f32[8,256]{1,0:T(8,128)S(1)}, f32[8,256]{1,0:T(8,128)S(1)}, f32[8,256]{1,0:T(8,128)S(1)}) custom-call(f32[8,256]{1,0:T(8,128)} %grad_h.1, f32[8,256]{1,0:T(8,128)} %warm_h.1, f32[32,8,256]{2,1,0:T(8,128)} %eta_h.1, f32[8,256]{1,0:T(8,128)} %coef_h.1, f32[2,8,256]{2,1,0:T(8,128)} %slide_h.1, ...), custom_call_target="tpu_custom_call" | custom-call | tf_op jit(solution)/shard_map/pallas_call | solution.py:579
  23.1 0.6 %multiply_subtract_fusion = (f32[8,256]{1,0:T(8,128)}, f32[8,256]{1,0:T(8,128)}) fusion(f32[8,256]{1,0:T(8,128)S(1)} %get-tuple-element.10, f32[8,256]{1,0:T(8,128)S(1)} %get-tuple-element.8, f32[8,256]{1,0:T(8,128)S(1)} %get-tuple-element.11, f32[8,256]{1,0:T(8,128)S(1)} %get-tuple-element.7, f32[8,256]{1,0:T(8,128)S(1)} %get-tuple-element.9), kind=kLoop, calls=%fused_computation | loop fusion | flops 8192 | bytes 57344 | tf_op jit(solution)/shard_map/sub | solution.py:580
